TPU v7x, 128 devices: a whole 4x4x4 slice. The times are simulated.
128 devices in a mesh: band: 16 (over x, y), sub: 8 (over z, core).
Axes of the slice: x: 4, y: 4, z: 4, core: 2. Of those that a mesh axis runs over, the one named last changes fastest.
Arguments:
- gas_amounts: bfloat16 [1024, 64, 8, 128], P('band'), may hold values from 0.049804688 to 1
- layer_mass: bfloat16 [1024, 64, 128], P('band'), may hold values from 4 to 40
- column_state: bfloat16 [1024, 2, 128], P('band'), may hold values from 0.099609375 to 0.796875
- absorption: bfloat16 [112, 8], P('sub'), may hold values from 0.0019989014 to 0.5
- single_scatter: float32 [112], P('sub'), may hold values from 0.2 to 0.95
- solar_weight: float32 [112], P('sub'), may hold values from 0.002 to 0.1
- sunlit: int32 [1024], replicated, may hold values from 0 to 1, as said below
Outputs:
- heating: float32 [1024, 64, 128], P(('band', 'sub'))
- surface_down: float32 [1024, 128], P(('band', 'sub'))
Inputs may be any that keep to these rules, and one draw needn't show every extreme that they name: Exactly 512 blocks are sunlit, and in every draw all 64 blocks of some band index are sunlit.
All inputs are finite; a program needn't handle non-finite values.
Results may differ from a plain program's by a relative error of at most 0.0003.
Values may be sent and summed in bfloat16 or wider, within the bound.
A program may use at most 192 MiB of HBM per device.

v0:
```python
import math

import jax
import jax.numpy as jnp
from jax import lax
from jax.sharding import PartitionSpec as P


def sent_together(arrays, axis, split_dim, concat_dim, along):
    widths = [math.prod(a.shape[along:]) for a in arrays]
    both = jnp.concatenate(
        [a.reshape(*a.shape[:along], w) for a, w in zip(arrays, widths)], axis=along
    )
    out = lax.all_to_all(both, axis, split_axis=split_dim, concat_axis=concat_dim, tiled=True)
    parts = jnp.split(out, [sum(widths[:k]) for k in range(1, len(widths))], axis=along)
    return tuple((b.reshape(*out.shape[:along], *a.shape[along:]) for a, b in zip(arrays, parts)))


def sent_together_2(arrays, axis, dim, along):
    columns = [a.reshape(*a.shape[:along], -1) for a in arrays]
    both = jnp.concatenate(columns, axis=along)
    out, at, gathered = (lax.all_gather(both, axis, axis=dim, tiled=True), 0, [])
    for a, column in zip(arrays, columns):
        slab = out[..., at : at + column.shape[along]]
        gathered.append(slab.reshape(*slab.shape[:along], *a.shape[along:]))
        at += column.shape[along]
    return tuple(gathered)


def in_blocks(x, dim, length):
    lengths = x.shape
    parts = x.reshape(*lengths[:dim], length, lengths[dim] // length, *lengths[dim + 1 :])
    return jnp.moveaxis(parts, dim, 0)


def summed_on_arrival(x, axis, dim):
    parts = in_blocks(x, dim, lax.axis_size(axis))
    arrived = lax.all_to_all(parts, axis, split_axis=0, concat_axis=0, tiled=True)
    return arrived.sum(axis=0)


def in_one_piece(arrays, axis, dim, along):
    columns = [a.reshape(*a.shape[:along], -1) for a in arrays]
    both = jnp.concatenate(columns, axis=along)
    out, at, gathered = (summed_on_arrival(both, axis, dim), 0, [])
    for a, column in zip(arrays, columns):
        slab = out[..., at : at + column.shape[along]]
        gathered.append(slab.reshape(*slab.shape[:along], *a.shape[along:]))
        at += column.shape[along]
    return tuple(gathered)


def layer_solve(optical, heat_factor, cosine, ground, single_scatter, solar_weight):
    omega = single_scatter[:, None]
    passing = jnp.exp(-optical)
    reflected = 0.5 * omega * (1.0 - passing * passing)
    unscattered = jnp.exp(-optical / cosine[None, None, :])

    def upward(lower_albedo, layer_data):
        reflect_now, pass_now = layer_data
        denominator = 1.0 - reflect_now * lower_albedo
        upper_albedo = reflect_now + pass_now * pass_now * lower_albedo / denominator
        return (upper_albedo, (upper_albedo, denominator))

    surface = jnp.broadcast_to(ground[None, :], optical.shape[1:])
    _, (stack_albedo, denominators) = lax.scan(
        upward, surface, (reflected, passing), reverse=True, unroll=8
    )

    def downward(state_now, layer_data):
        beam, diffuse = state_now
        albedo_now, pass_now, direct_now, denominator = layer_data
        net_flux = (1.0 - albedo_now) * (beam + diffuse)
        new_beam = beam * direct_now
        new_diffuse = (pass_now * diffuse + 0.5 * omega * (1.0 - direct_now) * beam) / denominator
        return ((new_beam, new_diffuse), jnp.sum(net_flux, axis=0))

    top_beam = solar_weight[:, None] * cosine[None, :]
    (beam, diffuse), net_sums = lax.scan(
        downward,
        (top_beam, jnp.zeros_like(top_beam)),
        (stack_albedo, passing, unscattered, denominators),
        unroll=8,
    )
    bottom_down = beam + diffuse
    bottom_net = jnp.sum((1.0 - ground[None, :]) * bottom_down, axis=0)
    interfaces = jnp.concatenate([net_sums, bottom_net[None, :]], axis=0)
    heating = heat_factor * (interfaces[:-1] - interfaces[1:])
    return (heating, jnp.sum(bottom_down, axis=0))


def pick_rows(array, index, lead_shape):
    return jnp.take(array, index, axis=0).reshape(lead_shape + array.shape[1:])


def compact(arrived, flat_slot):
    return jnp.take(
        arrived.reshape((arrived.shape[0] * arrived.shape[1],) + arrived.shape[2:]),
        flat_slot,
        axis=0,
    )


def body(gas_amounts, layer_mass, column_state, absorption, single_scatter, solar_weight, sunlit):
    band_count = lax.axis_size("band")
    sub_count = lax.axis_size("sub")
    band_index = lax.axis_index("band")
    sub_index = lax.axis_index("sub")
    owned, levels, gas_count, columns = gas_amounts.shape
    capacity = (owned + band_count - 1) // band_count
    helped = owned // 2
    before = jnp.cumsum(sunlit) - sunlit
    starts = before.reshape(band_count, owned)[:, 0]
    sunlit_mine = lax.dynamic_slice_in_dim(sunlit, band_index * owned, owned)
    my_rank = lax.dynamic_slice_in_dim(before, band_index * owned, owned)
    first_rank = starts[band_index]
    local_pos = my_rank - first_rank
    band_ids = jnp.arange(band_count, dtype=jnp.int32)
    block_ids = jnp.arange(owned, dtype=jnp.int32)
    per_dest = (capacity + sub_count - 1) // sub_count
    share = helped // sub_count
    lead_send = (band_count, per_dest)

    def first_turn(start_rank, dest):
        lowest = (start_rank - dest + band_count - 1) // band_count
        return lowest + jnp.mod(sub_index - lowest, sub_count)

    my_turn = first_turn(first_rank, band_ids)
    turns = my_turn[:, None] + jnp.arange(per_dest, dtype=jnp.int32)[None, :] * sub_count
    wanted = (turns * band_count + band_ids[:, None] - first_rank).reshape(-1)
    matches = (sunlit_mine[None, :] == 1) & (local_pos[None, :] == wanted[:, None])
    source_block = jnp.sum(jnp.where(matches, block_ids[None, :], 0), axis=1)
    arrived_gas, arrived_mass, arrived_state = sent_together(
        (
            pick_rows(gas_amounts, source_block, lead_send),
            pick_rows(layer_mass, source_block, lead_send),
            pick_rows(column_state, source_block, lead_send),
        ),
        "band",
        0,
        0,
        2,
    )
    helper_turn = sub_index + jnp.arange(share, dtype=jnp.int32) * sub_count
    sender = (
        jnp.sum(
            (starts[None, :] <= (helper_turn * band_count + band_index)[:, None]).astype(jnp.int32),
            axis=1,
        )
        - 1
    )
    flat_slot = (
        sender * per_dest + (helper_turn - first_turn(starts[sender], band_index)) // sub_count
    )
    got_gas = compact(arrived_gas, flat_slot)
    got_mass = compact(arrived_mass, flat_slot)
    got_state = compact(arrived_state, flat_slot)
    table_all, omega_all, weight_all = sent_together_2(
        (absorption.astype(jnp.float32), single_scatter, solar_weight), "sub", 0, 1
    )
    coefficients = table_all.astype(jnp.bfloat16)
    back_turn = (
        first_turn(starts, band_index)[:, None]
        + jnp.arange(per_dest, dtype=jnp.int32)[None, :] * sub_count
    )
    help_slot = jnp.clip((back_turn - sub_index) // sub_count, 0, share - 1).reshape(-1)
    own_dest = jnp.mod(my_rank, band_count)
    own_turn = my_rank // band_count
    own_first = jnp.sum(
        jnp.where(band_ids[None, :] == own_dest[:, None], my_turn[None, :], 0), axis=1
    )
    own_slot = jnp.clip(
        own_dest * per_dest + (own_turn - own_first) // sub_count, 0, band_count * per_dest - 1
    )
    own_keep = (sunlit_mine == 1) & (jnp.mod(own_turn, sub_count) == sub_index)
    solved = got_gas.shape[0]
    gpoint_share = coefficients.shape[0]
    optical = jnp.einsum("gs,plsc->lgpc", coefficients, got_gas, preferred_element_type=jnp.float32)
    optical = optical.reshape(levels, gpoint_share, solved * columns)
    heat_factor = (
        jnp.transpose(got_mass, (1, 0, 2)).reshape(levels, solved * columns).astype(jnp.float32)
    )
    cosine = got_state[:, 0, :].reshape(-1).astype(jnp.float32)
    ground = got_state[:, 1, :].reshape(-1).astype(jnp.float32)
    heating, surface_down = layer_solve(optical, heat_factor, cosine, ground, omega_all, weight_all)
    heating = jnp.transpose(heating.reshape(levels, solved, columns), (1, 0, 2))
    surface_down = surface_down.reshape(solved, columns)
    lead_back = (band_count, per_dest)
    heat_back, surface_back = sent_together(
        (pick_rows(heating, help_slot, lead_back), pick_rows(surface_down, help_slot, lead_back)),
        "band",
        0,
        0,
        2,
    )
    heat_own = compact(heat_back, own_slot)
    surface_own = compact(surface_back, own_slot)
    heat_own = jnp.where(own_keep[:, None, None], heat_own, jnp.zeros_like(heat_own))
    surface_own = jnp.where(own_keep[:, None], surface_own, jnp.zeros_like(surface_own))
    heating_out, surface_out = in_one_piece((heat_own, surface_own), "sub", 0, 1)
    return (heating_out, surface_out)


def solution(mesh):
    in_specs = (
        P("band", None, None, None),
        P("band", None, None),
        P("band", None, None),
        P("sub", None),
        P("sub"),
        P("sub"),
        P(),
    )
    out_specs = (P(("band", "sub"), None, None), P(("band", "sub"), None))
    return jax.shard_map(body, mesh=mesh, in_specs=in_specs, out_specs=out_specs, check_vma=False)
```

profile of v0, /device:TPU:1, one launch (start us, length us, event | category | flops | bytes accessed | tf_op | source)
XLA Modules:
  0.0 377.6 jit_solution(13097795137188372400)
XLA Ops:
  9.4 5.5 %gather_fusion.1 = bf16[16,64,8,128]{3,2,1,0:T(8,128)(2,1)} fusion(bf16[64,64,8,128]{3,2,1,0:T(8,128)(2,1)} %param.11, s32[1024]{0:T(1024)S(1)} %pad_clamp_fusion.3), kind=kCustom, calls=%fused_computation.1 | custom fusion | bytes 4194368 | tf_op jit(solution)/shard_map/jit(_take)/gather | solution.py:93
  15.0 2.1 gather.59
  18.0 3.1 reduce.15
  21.1 3.0 reshape.807
  24.2 7.7 %all-to-all-start = ((bf16[16,2,36992]{2,1,0:T(2,128)(2,1)}), bf16[16,2,36992]{2,1,0:T(2,128)(2,1)S(1)}, u32[]{:S(2)}, u32[]{:S(2)}) async-start(bf16[16,2,36992]{2,1,0:T(2,128)(2,1)} %reshape.807), calls=%async_computation | async-start | bytes 4734976 | tf_op jit(solution)/shard_map/all_to_all | solution.py:14
  33.8 14.7 %all-gather = f32[8,14,10]{2,1,0:T(8,128)S(1)} all-gather(f32[1,14,10]{2,1,0:T(8,128)S(1)} %copy.68), channel_id=1, replica_groups=mesh['band'=16,'sub'=8] {'sub'}, dimensions={0}, use_global_device_ids=true | all-gather | bytes 5040 | tf_op jit(solution)/shard_map/all_gather | solution.py:22
  50.0 13.8 %all-to-all-done = bf16[16,2,36992]{2,1,0:T(2,128)(2,1)S(1)} async-done(((bf16[16,2,36992]{2,1,0:T(2,128)(2,1)}), bf16[16,2,36992]{2,1,0:T(2,128)(2,1)S(1)}, u32[]{:S(2)}, u32[]{:S(2)}) %all-to-all-start) | async-done | bytes 2367520 | tf_op jit(solution)/shard_map/all_to_all | solution.py:14
  63.8 9.7 %reshape.808 = bf16[16,1,73984]{2,1,0:T(2,128)(2,1)} reshape(bf16[16,2,36992]{2,1,0:T(2,128)(2,1)S(1)} %all-to-all-done) | data formatting | bytes 4734976
  74.4 2.6 slice_reduce_fusion.1
  76.9 13.2 %slice_reduce_fusion = bf16[16,65536]{1,0:T(8,128)(2,1)S(1)} fusion(bf16[16,1,73984]{2,1,0:T(2,128)(2,1)} %reshape.808), kind=kLoop, calls=%fused_computation.178 | loop fusion | bytes 4194304 | tf_op jit(solution)/shard_map/split | solution.py:15
  92.5 2.2 gather_fusion.6
  95.5 2.1 negate_bitcast_fusion
  97.7 10.9 %copy.70 = f32[64,112,4,128]{3,2,1,0:T(4,128)} copy(f32[64,112,4,128]{3,1,0,2:T(8,128)S(1)} %negate_bitcast_fusion) | data formatting | bytes 29360128 | tf_op jit(solution)/shard_map/neg | solution.py:55
  108.6 17.5 %neg.15 = f32[8,8,112,512]{3,2,1,0:T(8,128)} reshape(f32[64,112,4,128]{3,2,1,0:T(4,128)} %copy.70) | data formatting | bytes 29360128 | tf_op jit(solution)/shard_map/neg | solution.py:55
  126.2 19.9 %subtract_multiply_fusion = (f32[8,8,112,512]{3,2,1,0:T(8,128)}, f32[8,8,112,512]{3,2,1,0:T(8,128)}, f32[8,8,112,512]{3,2,1,0:T(8,128)}) fusion(f32[112]{0:T(128)S(1)} %copy-done.13, f32[8,8,112,512]{3,2,1,0:T(8,128)} %neg.15, f32[512]{0:T(512)S(1)} %bitcast.590), kind=kLoop, calls=%fused_computation.175 | loop fusion | flops 14680064 | bytes 58722752 | tf_op jit(solution)/shard_map/mul | solution.py:56
  146.2 7.0 %broadcast.852.clone = f32[8,8,112,512]{3,2,1,0:T(8,128)} broadcast(f32[]{:T(128)} %constant.348.clone.1), dimensions={} | broadcast | bytes 14680068 | tf_op jit(solution)/shard_map/broadcast.97
  153.1 7.1 %broadcast.852 = f32[8,8,112,512]{3,2,1,0:T(8,128)} broadcast(f32[]{:T(128)} %constant.348.clone.1), dimensions={} | broadcast | bytes 14680068 | tf_op jit(solution)/shard_map/broadcast.97
  160.2 97.5 %while.33 = (s32[]{:T(128)}, f32[112,512]{1,0:T(8,128)S(1)}, f32[8,8,112,512]{3,2,1,0:T(8,128)}, f32[8,8,112,512]{3,2,1,0:T(8,128)}, f32[8,8,112,512]{3,2,1,0:T(...) while((s32[]{:T(128)}, f32[112,512]{1,0:T(8,128)S(1)}, ...), condition=%wide.region_6.7_spmd, body=%wide.region_5.6_spmd.sunk | while | flops 3670024 | bytes 22020432 | solution.py:66
  160.2 2.5 bitcast_dynamic-update-slice_fusion.36
  170.2 2.2 bitcast_dynamic-update-slice_fusion.51
  172.4 2.5 bitcast_dynamic-update-slice_fusion.36
  182.4 2.2 bitcast_dynamic-update-slice_fusion.51
  184.6 2.5 bitcast_dynamic-update-slice_fusion.36
  194.5 2.2 bitcast_dynamic-update-slice_fusion.51
  196.8 2.5 bitcast_dynamic-update-slice_fusion.36
  206.7 2.3 bitcast_dynamic-update-slice_fusion.51
  209.0 2.5 bitcast_dynamic-update-slice_fusion.36
  219.0 2.2 bitcast_dynamic-update-slice_fusion.51
  221.2 2.5 bitcast_dynamic-update-slice_fusion.36
  231.1 2.2 bitcast_dynamic-update-slice_fusion.51
  233.4 2.5 bitcast_dynamic-update-slice_fusion.36
  243.3 2.2 bitcast_dynamic-update-slice_fusion.51
  245.6 2.5 bitcast_dynamic-update-slice_fusion.36
  255.5 2.3 bitcast_dynamic-update-slice_fusion.51
  257.8 60.9 %while.34 = (s32[]{:T(128)}, f32[112,512]{1,0:T(8,128)S(1)}, f32[112,512]{1,0:T(8,128)S(1)}, f32[8,8,512]{2,1,0:T(8,128)S(1)}, f32[8,8,112,512]{3,2,1,0:T(8,128)...) while((s32[]{:T(128)}, f32[112,512]{1,0:T(8,128)S(1)}, ...), condition=%wide.region_16.17_spmd.clone, body=%wide.region_7.16_spmd.clone.sunk | while | flops 5099642 | bytes 13618127 | solution.py:79
  257.8 2.0 fusion.141
  259.8 2.3 fusion.142
  262.1 1.9 fusion.143
  265.4 2.0 fusion.141
  267.4 2.3 fusion.142
  269.7 1.9 fusion.143
  273.0 2.0 fusion.141
  275.0 2.3 fusion.142
  277.3 1.9 fusion.143
  280.6 2.0 fusion.141
  282.6 2.3 fusion.142
  284.9 1.9 fusion.143
  288.2 2.0 fusion.141
  290.2 2.3 fusion.142
  292.5 1.9 fusion.143
  295.8 2.0 fusion.141
  297.8 2.3 fusion.142
  300.1 1.9 fusion.143
  303.5 2.0 fusion.141
  305.4 2.3 fusion.142
  307.7 1.9 fusion.143
  311.1 2.0 fusion.141
  313.0 2.3 fusion.142
  315.4 1.9 fusion.143
  322.3 3.6 all-to-all-start.1
  326.2 8.7 %all-to-all-done.1 = f32[16,1,8320]{2,1,0:T(1,128)S(1)} async-done(((f32[16,1,8320]{2,1,0:T(1,128)}), f32[16,1,8320]{2,1,0:T(1,128)S(1)}, u32[]{:S(2)}, u32[]{:S(2)}) %all-to-all-start.1) | async-done | bytes 532512 | tf_op jit(solution)/shard_map/all_to_all | solution.py:14
  335.6 2.0 gather_fusion.9
  337.6 1.7 gather.72
  339.9 36.2 %all_to_all.15 = f32[8,8,8320]{2,1,0:T(8,128)S(1)} all-to-all(f32[8,8,8320]{2,1,0:T(8,128)S(1)} %pad_maximum_fusion.1), channel_id=1, replica_groups=mesh['band'=16,'sub'=8] {'sub'}, dimensions={0} | all-to-all | bytes 4259840 | tf_op jit(solution)/shard_map/all_to_all | solution.py:38
  (260 shorter events, 93.2 us)
Async XLA Ops:
  0.6 7.9 %copy-start = (bf16[64,64,128]{2,1,0:T(8,128)(2,1)S(1)}, bf16[64,64,128]{2,1,0:T(8,128)(2,1)}, u32[]{:S(2)}) copy-start(bf16[64,64,128]{2,1,0:T(8,128)(2,1)} %param.12) | copy-start | bytes 3145732
  2.8 5.7 %copy-start.3 = (s32[16,64]{1,0:T(8,128)}, s32[16,64]{1,0:T(8,128)S(1)}, u32[]{:S(2)}) copy-start(s32[16,64]{1,0:T(8,128)S(1)} %reshape.695) | copy-start | bytes 12292
  24.2 7.8 %copy-start.10 = (bf16[14,8]{0,1:T(8,128)(2,1)S(1)}, bf16[14,8]{0,1:T(8,128)(2,1)}, u32[]{:S(2)}) copy-start(bf16[14,8]{0,1:T(8,128)(2,1)} %param.14) | copy-start | bytes 676
  24.2 7.8 %copy-start.17 = (f32[14]{0:T(128)S(1)}, f32[14]{0:T(128)}, u32[]{:S(2)}) copy-start(f32[14]{0:T(128)} %param.16) | copy-start | bytes 172
  24.2 7.8 %copy-start.18 = (f32[14]{0:T(128)S(1)}, f32[14]{0:T(128)}, u32[]{:S(2)}) copy-start(f32[14]{0:T(128)} %param.15) | copy-start | bytes 172
  24.2 7.9 %copy-start.4 = (s32[16,64]{1,0:T(8,128)S(1)}, s32[16,64]{1,0:T(8,128)}, u32[]{:S(2)}) copy-start(s32[16,64]{1,0:T(8,128)} %copy-done.3) | copy-start | bytes 12292
  24.2 39.7 %all-to-all-start = ((bf16[16,2,36992]{2,1,0:T(2,128)(2,1)}), bf16[16,2,36992]{2,1,0:T(2,128)(2,1)S(1)}, u32[]{:S(2)}, u32[]{:S(2)}) async-start(bf16[16,2,36992]{2,1,0:T(2,128)(2,1)} %reshape.807), calls=%async_computation | async-start | bytes 4734976 | tf_op jit(solution)/shard_map/all_to_all | solution.py:14
  48.7 24.8 %copy-start.5 = (f32[112,10]{0,1:T(8,128)}, f32[112,10]{0,1:T(8,128)S(1)}, u32[]{:S(2)}) copy-start(f32[112,10]{0,1:T(8,128)S(1)} %reshape.797) | copy-start | bytes 13444
  49.4 43.2 %copy-start.7 = (s32[1024]{0:T(1024)}, s32[1024]{0:T(1024)S(1)}, u32[]{:S(2)}) copy-start(s32[1024]{0:T(1024)S(1)} %pad_clamp_fusion.2) | copy-start | bytes 12292
  90.8 4.7 %copy-start.6 = (f32[112,10]{0,1:T(8,128)S(1)}, f32[112,10]{0,1:T(8,128)}, u32[]{:S(2)}) copy-start(f32[112,10]{0,1:T(8,128)} %copy-done.5) | copy-start | bytes 13444
  108.6 17.6 %copy-start.9 = (f32[112]{0:T(128)S(1)}, f32[112]{0:T(128)}, u32[]{:S(2)}) copy-start(f32[112]{0:T(128)} %get-tuple-element.288) | copy-start | bytes 1348
  108.6 17.6 %copy-start.13 = (f32[112]{0:T(128)S(1)}, f32[112]{0:T(128)}, u32[]{:S(2)}) copy-start(f32[112]{0:T(128)} %get-tuple-element.286) | copy-start | bytes 1348
  160.2 97.5 %copy-start.2 = (f32[112,512]{1,0:T(8,128)S(1)}, f32[112,512]{1,0:T(8,128)}, u32[]{:S(2)}) copy-start(f32[112,512]{1,0:T(8,128)} %custom-call) | copy-start | bytes 688132
  160.2 97.5 %copy-start.14 = (f32[112,1]{0,1:T(1,128)S(1)}, f32[112,1]{0,1:T(1,128)}, u32[]{:S(2)}) copy-start(f32[112,1]{0,1:T(1,128)} %get-tuple-element.509) | copy-start | bytes 1348
  257.8 62.5 %copy-start.8 = (pred[16]{0:T(512)(128)(4,1)S(1)}, pred[16]{0:T(512)(128)(4,1)}, u32[]{:S(2)}) copy-start(pred[16]{0:T(512)(128)(4,1)} %get-tuple-element.276) | copy-start | bytes 52
  319.5 6.4 %copy-start.12 = (s32[64]{0:T(128)S(1)}, s32[64]{0:T(128)}, u32[]{:S(2)}) copy-start(s32[64]{0:T(128)} %get-tuple-element.272) | copy-start | bytes 772
  319.5 6.4 %copy-start.16 = (pred[64]{0:T(512)(128)(4,1)S(1)}, pred[64]{0:T(512)(128)(4,1)}, u32[]{:S(2)}) copy-start(pred[64]{0:T(512)(128)(4,1)} %get-tuple-element.270) | copy-start | bytes 196
  319.5 6.5 %copy-start.15 = (s32[16]{0:T(128)S(1)}, s32[16]{0:T(128)}, u32[]{:S(2)}) copy-start(s32[16]{0:T(128)} %get-tuple-element.293) | copy-start | bytes 196
  319.5 6.6 %copy-start.11 = (s32[64]{0:T(128)S(1)}, s32[64]{0:T(128)}, u32[]{:S(2)}) copy-start(s32[64]{0:T(128)} %get-tuple-element.271) | copy-start | bytes 772
  322.3 12.6 %all-to-all-start.1 = ((f32[16,1,8320]{2,1,0:T(1,128)}), f32[16,1,8320]{2,1,0:T(1,128)S(1)}, u32[]{:S(2)}, u32[]{:S(2)}) async-start(f32[16,1,8320]{2,1,0:T(1,128)} %pad_maximum_fusion.2), calls=%async_computation.1 | async-start | bytes 1064960 | tf_op jit(solution)/shard_map/all_to_all | solution.py:14
  339.9 37.7 %copy-start.1 = (bf16[64,64,128]{2,1,0:T(8,128)(2,1)S(1)}, bf16[64,64,128]{2,1,0:T(8,128)(2,1)}, u32[]{:S(2)}) copy-start(bf16[64,64,128]{2,1,0:T(8,128)(2,1)} %param.12) | copy-start | bytes 3145732
where the time goes:
time: 382 us; the launch traced here: 378 us
  other arithmetic  173 us (45%)
  local copies, waits for them, and re-layouts  116 us (30%)
  blocking collectives  50.9 us (13%)
  waiting for transfers between devices  22.5 us (6%)
  starting transfers between devices  11.3 us (3%)
    while x64, other arithmetic  77.9 us
    all_to_all x1, blocking collectives, summed_on_arrival(): lax.all_to_all(parts, axis, split_axis=0, concat_axis=0, tiled=True)  36.2 us
    reduce_sum x16, other arithmetic, downward(): return ((new_beam, new_diffuse), jnp.sum(net_flux, axis=0))  31.4 us
    div x16, other arithmetic, downward(): (pass_now * diffuse + 0.5 * omega * (1.0 - direct_now) * beam) / denominator  28.8 us
    neg x2, local copies, waits for them, and re-layouts, layer_solve(): passing = jnp.exp(-optical)  28.5 us
    all_to_all x2, waiting for transfers between devices, sent_together(): lax.all_to_all(both, axis, split_axis=split_dim, concat_axis=concat_dim,...  22.5 us
    mul x2, other arithmetic, layer_solve(): reflected = 0.5 * omega * (1.0 - passing * passing)  20.5 us
    dynamic_update_slice x8, local copies, waits for them, and re-layouts, layer_solve(): lax.scan(upward, surface, (reflected, passing), reverse=True, unroll=8)  18 us
  transfers between devices with their start and end apart: 2, of which 2 were waited for; matrix products, arithmetic and copies ran while one was open for 1% of the time, Pallas kernels for 0%

commit v1 on v0

v1 whole, which is shorter than its diff:
```python
import functools
import math

import jax
import jax.numpy as jnp
from jax import lax
from jax.experimental import pallas as pl
from jax.experimental.pallas import tpu as pltpu
from jax.sharding import PartitionSpec as P

MESH = pl.DeviceIdType.MESH
LOG2E = math.log2(math.e)
CHUNK = 8


def gather_kernel(subs, table_ref, omega_ref, weight_ref, table_out, omega_out, weight_out, send_sem, recv_sem):
    band = lax.axis_index("band")
    sub = lax.axis_index("sub")
    barrier = pltpu.get_barrier_semaphore()
    for step in range(1, subs):
        pl.semaphore_signal(barrier, inc=1, device_id=(band, lax.rem(sub + step, subs)), device_id_type=MESH)
    pl.semaphore_wait(barrier, subs - 1)
    pairs = ((table_ref, table_out), (omega_ref, omega_out), (weight_ref, weight_out))
    copies = []
    for step in range(1, subs):
        peer = lax.rem(sub + step, subs)
        for k, (source, target) in enumerate(pairs):
            copy = pltpu.make_async_remote_copy(
                src_ref=source,
                dst_ref=target.at[sub],
                send_sem=send_sem.at[step, k],
                recv_sem=recv_sem.at[step, k],
                device_id=(band, peer),
                device_id_type=MESH,
            )
            copy.start()
            copies.append(copy)
    for source, target in pairs:
        target[sub] = source[...]
    for copy in copies:
        copy.wait()


def gather_tables(absorption, single_scatter, solar_weight, subs):
    share, gases = absorption.shape
    vmem = pl.BlockSpec(memory_space=pltpu.VMEM)
    return pl.pallas_call(
        functools.partial(gather_kernel, subs),
        out_shape=(
            jax.ShapeDtypeStruct((subs, share, gases), jnp.bfloat16),
            jax.ShapeDtypeStruct((subs, 1, share), jnp.float32),
            jax.ShapeDtypeStruct((subs, 1, share), jnp.float32),
        ),
        in_specs=[vmem] * 3,
        out_specs=[vmem] * 3,
        scratch_shapes=[pltpu.SemaphoreType.DMA((subs, 3)), pltpu.SemaphoreType.DMA((subs, 3))],
        compiler_params=pltpu.CompilerParams(collective_id=0, has_side_effects=True),
        name="gather_tables",
    )(absorption, single_scatter.reshape(1, share), solar_weight.reshape(1, share))


def as_column(row, length):
    square = jnp.broadcast_to(row, (length, length))
    rows = lax.broadcasted_iota(jnp.int32, (length, length), 0)
    cols = lax.broadcasted_iota(jnp.int32, (length, length), 1)
    return jnp.sum(jnp.where(rows == cols, square, 0.0), axis=1, keepdims=True)


def solve_kernel(
    own, levels, gases, columns, gpoints, subs,
    sunlit_ref, table_ref, omega_ref, weight_ref, gas_hbm, mass_hbm, state_hbm,
    heat_ref, surf_ref,
    gas_v, mass_v, state_v, coef_v, half_v, weight_v, spread_v,
    depth_v, pass_v, albedo_v, inverse_v, net_v, sem,
):
    band = lax.axis_index("band")
    sub = lax.axis_index("sub")
    share = gpoints // subs
    first = sub * own
    inputs = ((gas_hbm, gas_v), (mass_hbm, mass_v), (state_hbm, state_v))
    copies = [
        pltpu.make_async_copy(source.at[pl.ds(first, own)], target, sem.at[k])
        for k, (source, target) in enumerate(inputs)
    ]
    for copy in copies:
        copy.start()

    for s in range(subs):
        rows = pl.ds(s * share, share)
        coef_v[rows, :] = table_ref[s].astype(jnp.float32) * (-LOG2E)
        half_v[rows, :] = jnp.broadcast_to(0.5 * as_column(omega_ref[s], share), (share, columns))
        weight_v[rows, :] = jnp.broadcast_to(as_column(weight_ref[s], share), (share, columns))
    coef = coef_v[...]
    high = coef.astype(jnp.bfloat16)
    rest = coef - high.astype(jnp.float32)
    middle = rest.astype(jnp.bfloat16)
    low = (rest - middle.astype(jnp.float32)).astype(jnp.bfloat16)
    width = CHUNK * gases
    spread_v[...] = jnp.zeros_like(spread_v)
    for k, part in enumerate((high, middle, low)):
        for l in range(CHUNK):
            at = k * width + l * gases
            spread_v[pl.ds(l * gpoints, gpoints), at : at + gases] = part
    for copy in copies:
        copy.wait()

    chunks = levels // CHUNK

    def block(j, carry):
        state = state_v[j].astype(jnp.float32)
        mu = state[0:1, :]
        ground = state[1:2, :]
        slant = jnp.broadcast_to(1.0 / mu, (8, columns))
        slant = jnp.broadcast_to(slant[0:1, :], (gpoints, columns))

        def optical(c):
            amounts = gas_v[j, pl.ds(pl.multiple_of(c * width, width), width), :]
            amounts = jnp.concatenate([amounts] * 3, axis=0)
            depth = jnp.dot(spread_v[...], amounts, preferred_element_type=jnp.float32)
            depth_v[pl.ds(c * CHUNK, CHUNK)] = depth.reshape(CHUNK, gpoints, columns)

        def upward(i, albedo):
            c = chunks - 1 - i
            optical(c)
            for k in range(CHUNK - 1, -1, -1):
                l = c * CHUNK + k
                half = half_v[...]
                passing = jnp.exp2(depth_v[l])
                square = passing * passing
                reflected = half - half * square
                inverse = 1.0 / (1.0 - reflected * albedo)
                albedo = reflected + square * (albedo * inverse)
                pass_v[l] = passing
                albedo_v[l] = albedo
                inverse_v[l] = inverse
            return albedo

        surface = jnp.broadcast_to(ground, (gpoints, columns))
        lax.fori_loop(0, chunks, upward, surface)

        def downward(c, carry):
            beam, diffuse = carry
            for k in range(CHUNK):
                l = c * CHUNK + k
                half = half_v[...]
                total = (1.0 - albedo_v[l]) * (beam + diffuse)
                net_v[pl.ds(pl.multiple_of(l * 8, 8), 8), :] = jnp.sum(
                    total.reshape(gpoints // 8, 8, columns), axis=0
                )
                beam_next = beam * jnp.exp2(depth_v[l] * slant)
                diffuse = (pass_v[l] * diffuse + half * (beam - beam_next)) * inverse_v[l]
                beam = beam_next
            return beam, diffuse

        top = weight_v[...] * jnp.broadcast_to(mu, (gpoints, columns))
        beam, diffuse = lax.fori_loop(0, chunks, downward, (top, jnp.zeros_like(top)))
        down = jnp.sum((beam + diffuse).reshape(gpoints // 8, 8, columns), axis=0)
        net_v[pl.ds(levels * 8, 8), :] = down * (1.0 - jnp.broadcast_to(ground, (8, columns)))
        here = net_v[pl.ds(0, levels, stride=8), :]
        below = net_v[pl.ds(8, levels, stride=8), :]
        for s in range(1, 8):
            here = here + net_v[pl.ds(s, levels, stride=8), :]
            below = below + net_v[pl.ds(8 + s, levels, stride=8), :]
        lit = sunlit_ref[(band * subs + sub) * own + j] == 1
        heating = mass_v[j].astype(jnp.float32) * (here - below)
        heat_ref[j] = jnp.where(lit, heating, jnp.zeros_like(heating))
        surface_down = jnp.sum(down, axis=0, keepdims=True)
        surf_ref[pl.ds(j, 1), :] = jnp.where(lit, surface_down, jnp.zeros_like(surface_down))
        return carry

    lax.fori_loop(0, own, block, 0)


def solve(gas_amounts, layer_mass, column_state, tables, sunlit, subs):
    blocks, levels, gases, columns = gas_amounts.shape
    own = blocks // subs
    gpoints = tables[0].shape[0] * tables[0].shape[1]
    vmem = pl.BlockSpec(memory_space=pltpu.VMEM)
    anywhere = pl.BlockSpec(memory_space=pl.ANY)
    per_level = pltpu.VMEM((levels, gpoints, columns), jnp.float32)
    return pl.pallas_call(
        functools.partial(solve_kernel, own, levels, gases, columns, gpoints, subs),
        out_shape=(
            jax.ShapeDtypeStruct((own, levels, columns), jnp.float32),
            jax.ShapeDtypeStruct((own, columns), jnp.float32),
        ),
        in_specs=[pl.BlockSpec(memory_space=pltpu.SMEM)] + [vmem] * 3 + [anywhere] * 3,
        out_specs=[vmem] * 2,
        scratch_shapes=[
            pltpu.VMEM((own, levels * gases, columns), jnp.bfloat16),
            pltpu.VMEM((own, levels, columns), jnp.bfloat16),
            pltpu.VMEM((own, 2, columns), jnp.bfloat16),
            pltpu.VMEM((gpoints, gases), jnp.float32),
            pltpu.VMEM((gpoints, columns), jnp.float32),
            pltpu.VMEM((gpoints, columns), jnp.float32),
            pltpu.VMEM((CHUNK * gpoints, 3 * CHUNK * gases), jnp.bfloat16),
            per_level, per_level, per_level, per_level,
            pltpu.VMEM(((levels + 1) * 8, columns), jnp.float32),
            pltpu.SemaphoreType.DMA((3,)),
        ],
        compiler_params=pltpu.CompilerParams(vmem_limit_bytes=48 * 1024 * 1024),
        name="solve_blocks",
    )(sunlit, *tables, gas_amounts.reshape(blocks, levels * gases, columns), layer_mass, column_state)


def body(gas_amounts, layer_mass, column_state, absorption, single_scatter, solar_weight, sunlit):
    subs = lax.axis_size("sub")
    tables = gather_tables(absorption, single_scatter, solar_weight, subs)
    return solve(gas_amounts, layer_mass, column_state, tables, sunlit, subs)


def solution(mesh):
    in_specs = (
        P("band", None, None, None),
        P("band", None, None),
        P("band", None, None),
        P("sub", None),
        P("sub"),
        P("sub"),
        P(),
    )
    out_specs = (P(("band", "sub"), None, None), P(("band", "sub"), None))
    return jax.shard_map(body, mesh=mesh, in_specs=in_specs, out_specs=out_specs, check_vma=False)
```

time: 382 us -> 59.9 us (0.16); the launches traced: 378 us -> 59.4 us
  other arithmetic: 173 us -> 0 us
  local copies, waits for them, and re-layouts: 116 us -> 6.13 us
  Pallas kernels: 0 us -> 52.6 us
  blocking collectives: 50.9 us -> 0 us
  waiting for transfers between devices: 22.5 us -> 0 us
  starting transfers between devices: 11.3 us -> 0 us
    while x64 -> x0, other arithmetic: 77.9 us -> none
    pallas_call x0 -> x2, Pallas kernels: none -> 52.6 us  [the longest x1 42.5 us: solve(): pl.pallas_call(functools.partial(solve_kernel, own, levels, gases, column...]
    all_to_all x1 -> x0, blocking collectives: 36.2 us -> none  [summed_on_arrival(): lax.all_to_all(parts, axis, split_axis=0, concat_axis=0, tiled=True)]
    reduce_sum x21 -> x0, other arithmetic: 32 us -> none  [the longest x16 31.4 us: downward(): return ((new_beam, new_diffuse), jnp.sum(net_flux, axis=0))]
    div x16 -> x0, other arithmetic: 28.8 us -> none  [downward(): (pass_now * diffuse + 0.5 * omega * (1.0 - direct_now) * beam) / denominator]
    neg x2 -> x0, local copies, waits for them, and re-layouts: 28.5 us -> none  [layer_solve(): passing = jnp.exp(-optical)]
    all_to_all x2 -> x0, waiting for transfers between devices: 22.5 us -> none  [sent_together(): lax.all_to_all(both, axis, split_axis=split_dim, concat_axis=concat_dim,...]
    mul x11 -> x0, other arithmetic: 20.6 us -> none  [the longest x2 20.5 us: layer_solve(): reflected = 0.5 * omega * (1.0 - passing * passing)]
  transfers between devices with their start and end apart: 2 -> 0, of which waited for: 2 -> 0; matrix products, arithmetic and copies ran while one was open for 1% -> 0% of each run, Pallas kernels for 0% -> 0%
where the time goes in v1:
time: 59.9 us; the launch traced here: 59.4 us
  Pallas kernels  52.6 us (88%)
  local copies, waits for them, and re-layouts  6.13 us (10%)
  between operations  0.65 us (1%)
    pallas_call x1, Pallas kernels, solve(): pl.pallas_call(functools.partial(solve_kernel, own, levels, gases, column...  42.5 us
    pallas_call x1, Pallas kernels, gather_tables(): pl.pallas_call(functools.partial(gather_kernel, subs), out_shape=(jax.Sha...  10.1 us
    unnamed x13, local copies, waits for them, and re-layouts  6.13 us

profile of v1, /device:TPU:1, one launch (start us, length us, event | category | flops | bytes accessed | tf_op | source)
XLA Modules:
  0.0 59.4 jit_solution(5102952937193713553)
XLA Ops:
  0.6 1.4 %copy.9.table_ref = bf16[14,8]{1,0:T(8,128)(2,1)} copy(bf16[14,8]{0,1:T(8,128)(2,1)} %param.10) | data formatting | bytes 448 | tf_op args[3]
  2.0 10.1 %gather_tables.1 = (bf16[8,14,8]{2,1,0:T(8,128)(2,1)}, f32[8,1,14]{2,1,0:T(1,128)}, f32[8,1,14]{2,1,0:T(1,128)}) custom-call(bf16[14,8]{1,0:T(8,128)(2,1)} %copy.9.table_ref, f32[1,14]{1,0:T(1,128)} %bitcast.4, f32[1,14]{1,0:T(1,128)} %bitcast.5), custom_call_target="tpu_custom_call" | custom-call | tf_op jit(solution)/shard_map/gather_tables/pallas_call | solution.py:47
  12.1 0.0 copy-start
  12.1 1.2 %copy-done = bf16[64,64,128]{2,1,0:T(8,128)(2,1)S(1)} copy-done((bf16[64,64,128]{2,1,0:T(8,128)(2,1)S(1)}, bf16[64,64,128]{2,1,0:T(8,128)(2,1)}, u32[]{:S(2)}) %copy-start) | copy-done | bytes 1048600
  13.3 0.0 copy-start.1
  13.3 0.8 %copy-done.1 = bf16[64,2,128]{2,1,0:T(2,128)(2,1)S(1)} copy-done((bf16[64,2,128]{2,1,0:T(2,128)(2,1)S(1)}, bf16[64,2,128]{2,1,0:T(2,128)(2,1)}, u32[]{:S(2)}) %copy-start.1) | copy-done | bytes 32792
  14.1 0.0 copy-start.2
  14.1 0.8 %copy-done.2 = bf16[8,14,8]{2,1,0:T(8,128)(2,1)S(1)} copy-done((bf16[8,14,8]{2,1,0:T(8,128)(2,1)S(1)}, bf16[8,14,8]{2,1,0:T(8,128)(2,1)}, u32[]{:S(2)}) %copy-start.2) | copy-done | bytes 1816
  14.8 0.0 copy-start.3
  14.8 0.7 %copy-done.3 = s32[1024]{0:T(1024)S(1)} copy-done((s32[1024]{0:T(1024)S(1)}, s32[1024]{0:T(1024)}, u32[]{:S(2)}) %copy-start.3) | copy-done | bytes 4120
  15.5 0.0 copy-start.4
  15.5 0.7 %copy-done.4 = f32[8,1,14]{2,1,0:T(1,128)S(1)} copy-done((f32[8,1,14]{2,1,0:T(1,128)S(1)}, f32[8,1,14]{2,1,0:T(1,128)}, u32[]{:S(2)}) %copy-start.4) | copy-done | bytes 472
  16.2 0.0 copy-start.5
  16.2 0.7 %copy-done.5 = f32[8,1,14]{2,1,0:T(1,128)S(1)} copy-done((f32[8,1,14]{2,1,0:T(1,128)S(1)}, f32[8,1,14]{2,1,0:T(1,128)}, u32[]{:S(2)}) %copy-start.5) | copy-done | bytes 472
  16.9 42.5 %solve_blocks.1 = (f32[8,64,128]{2,1,0:T(8,128)}, f32[8,128]{1,0:T(8,128)}) custom-call(s32[1024]{0:T(1024)S(1)} %copy-done.3, bf16[8,14,8]{2,1,0:T(8,128)(2,1)S(1)} %copy-done.2, f32[8,1,14]{2,1,0:T(1,128)S(1)} %copy-done.4, f32[8,1,14]{2,1,0:T(1,128)S(1)} %copy-done.5, bf16[64,512,128]{2,1,0:T(8,128)(2,1)} %bitcast.3, bf16[64,64,128]{2,1,0:T(8,128)(2,1)S(1)} %copy-done, ...), custom_call_target="tpu_custom_call" | custom-call | tf_op jit(solution)/shard_map/solve_blocks/pallas_call | solution.py:181
Async XLA Ops:
  12.1 1.2 %copy-start = (bf16[64,64,128]{2,1,0:T(8,128)(2,1)S(1)}, bf16[64,64,128]{2,1,0:T(8,128)(2,1)}, u32[]{:S(2)}) copy-start(bf16[64,64,128]{2,1,0:T(8,128)(2,1)} %mass_hbm.1) | copy-start | bytes 3145732
  13.3 0.8 %copy-start.1 = (bf16[64,2,128]{2,1,0:T(2,128)(2,1)S(1)}, bf16[64,2,128]{2,1,0:T(2,128)(2,1)}, u32[]{:S(2)}) copy-start(bf16[64,2,128]{2,1,0:T(2,128)(2,1)} %state_hbm.1) | copy-start | bytes 98308
  14.1 0.8 %copy-start.2 = (bf16[8,14,8]{2,1,0:T(8,128)(2,1)S(1)}, bf16[8,14,8]{2,1,0:T(8,128)(2,1)}, u32[]{:S(2)}) copy-start(bf16[8,14,8]{2,1,0:T(8,128)(2,1)} %get-tuple-element.5.table_ref) | copy-start | bytes 5380
  14.8 0.7 %copy-start.3 = (s32[1024]{0:T(1024)S(1)}, s32[1024]{0:T(1024)}, u32[]{:S(2)}) copy-start(s32[1024]{0:T(1024)} %sunlit_ref.1) | copy-start | bytes 12292
  15.5 0.7 %copy-start.4 = (f32[8,1,14]{2,1,0:T(1,128)S(1)}, f32[8,1,14]{2,1,0:T(1,128)}, u32[]{:S(2)}) copy-start(f32[8,1,14]{2,1,0:T(1,128)} %get-tuple-element.6.omega_ref) | copy-start | bytes 1348
  16.2 0.7 %copy-start.5 = (f32[8,1,14]{2,1,0:T(1,128)S(1)}, f32[8,1,14]{2,1,0:T(1,128)}, u32[]{:S(2)}) copy-start(f32[8,1,14]{2,1,0:T(1,128)} %get-tuple-element.7.weight_ref) | copy-start | bytes 1348

commit v2 on v1

v2 whole, which is shorter than its diff:
```python
import functools
import math

import jax
import jax.numpy as jnp
from jax import lax
from jax.experimental import pallas as pl
from jax.experimental.pallas import tpu as pltpu
from jax.sharding import PartitionSpec as P

MESH = pl.DeviceIdType.MESH
LOG2E = math.log2(math.e)
CHUNK = 8
STEP = 16
UP = 4


def kernel(
    own, levels, gases, columns, gpoints, subs,
    gas_hbm, mass_hbm, state_hbm, table_hbm, omega_hbm, weight_hbm, sunlit_hbm,
    heat_hbm, surf_hbm,
    sunlit_s, gas_v, mass_v, state_v, table_v, omega_v, weight_v, lay_v, half_v, top_v, spread_v, coef_v,
    depth_0, depth_1, pass_v, albedo_v, inverse_v, net_v, flux_v, heat_v, surf_v,
    gas_sem, in_sem, out_sem, send_sem, recv_sem,
):
    band = lax.axis_index("band")
    sub = lax.axis_index("sub")
    share = gpoints // subs
    tiles = gpoints // 8
    steps = levels // STEP
    dots = STEP // CHUNK
    width = CHUNK * gases
    first = sub * own

    tables = ((table_hbm, table_v), (omega_hbm, omega_v), (weight_hbm, weight_v))
    own_tables = [
        pltpu.make_async_copy(source, target.at[sub], in_sem.at[k]) for k, (source, target) in enumerate(tables)
    ]
    for copy in own_tables:
        copy.start()
    barrier = pltpu.get_barrier_semaphore()
    for step in range(1, subs):
        pl.semaphore_signal(barrier, inc=1, device_id=(band, lax.rem(sub + step, subs)), device_id_type=MESH)

    def gas_copy(j):
        return pltpu.make_async_copy(gas_hbm.at[first + j], gas_v.at[j], gas_sem.at[j])

    others = [
        pltpu.make_async_copy(state_hbm.at[pl.ds(first, own)], state_v, in_sem.at[3]),
        pltpu.make_async_copy(mass_hbm.at[pl.ds(first, own)], mass_v, in_sem.at[4]),
        pltpu.make_async_copy(sunlit_hbm, sunlit_s, in_sem.at[5]),
    ]
    for j in range(own):
        gas_copy(j).start()
    for copy in others:
        copy.start()
    lay_v[...] = jnp.zeros_like(lay_v)
    spread_v[...] = jnp.zeros_like(spread_v)
    for copy in own_tables:
        copy.wait()
    pl.semaphore_wait(barrier, subs - 1)
    sent = []
    for step in range(1, subs):
        for k, (_, held) in enumerate(tables):
            copy = pltpu.make_async_remote_copy(
                src_ref=held.at[sub],
                dst_ref=held.at[sub],
                send_sem=send_sem.at[step, k],
                recv_sem=recv_sem.at[step, k],
                device_id=(band, lax.rem(sub + step, subs)),
                device_id_type=MESH,
            )
            copy.start()
            sent.append(copy)
    for copy in others:
        copy.wait()
    gas_copy(0).wait()
    for copy in sent:
        copy.wait()

    for s in range(subs):
        at = slice(s * share, (s + 1) * share)
        lay_v[0:gases, at] = table_v[s].astype(jnp.float32)
        lay_v[gases : gases + 1, at] = omega_v[s]
        lay_v[gases + 1 : gases + 2, at] = weight_v[s]
    by_row = jnp.transpose(lay_v[...])[:gpoints]
    coef = by_row[:, :gases] * (-LOG2E)
    half_v[...] = jnp.broadcast_to(0.5 * by_row[:, gases : gases + 1], (gpoints, columns))
    top_v[...] = jnp.broadcast_to(by_row[:, gases + 1 : gases + 2], (gpoints, columns))
    high = coef.astype(jnp.bfloat16).astype(jnp.float32)
    middle = (coef - high).astype(jnp.bfloat16).astype(jnp.float32)
    low = coef - high - middle
    for k, part in enumerate((high, middle, low)):
        for l in range(CHUNK):
            at = k * width + l * gases
            spread_v[pl.ds(l * gpoints, gpoints), at : at + gases] = part
    coef_v[...] = spread_v[...].astype(jnp.bfloat16)

    depths = (depth_0, depth_1)

    def state_row(j, k):
        row = state_v[j].astype(jnp.float32)[k : k + 1, :]
        return jnp.broadcast_to(row, (8, columns))

    def all_rows(row):
        return jnp.broadcast_to(row[None], (tiles, 8, columns)).reshape(gpoints, columns)

    def optical(j, slot, i):
        amounts = jnp.concatenate(
            [gas_v[j, pl.ds(pl.multiple_of((i * dots + d) * width, width), width), :] for d in range(dots)], axis=1
        )
        amounts = jnp.concatenate([amounts] * 3, axis=0)
        depth = jnp.dot(coef_v[...], amounts, preferred_element_type=jnp.float32)
        for d in range(dots):
            for m in range(CHUNK):
                part = depth[m * gpoints : (m + 1) * gpoints, d * columns : (d + 1) * columns]
                depths[slot][i * STEP + d * CHUNK + m] = part

    def upward(j, slot):
        def body(i, albedo):
            half = half_v[...]
            for k in range(UP):
                l = levels - 1 - (i * UP + k)
                passing = jnp.exp2(depths[slot][l])
                pass_v[l] = passing
                square = passing * passing
                reflected = half - half * square
                inverse = 1.0 / (1.0 - reflected * albedo)
                albedo = reflected + (square * albedo) * inverse
                albedo_v[l] = albedo
                inverse_v[l] = inverse
            return albedo

        lax.fori_loop(0, levels // UP, body, all_rows(state_row(j, 1)))

    def downward(j, slot, j_next):
        top = top_v[...] * all_rows(state_row(j, 0))
        slant = all_rows(1.0 / state_row(j, 0))

        def body(i, carry):
            beam, diffuse = carry
            half = half_v[...]
            if j_next is not None:
                optical(j_next, 1 - slot, i)
            for k in range(STEP):
                l = i * STEP + k
                net = (1.0 - albedo_v[l]) * (beam + diffuse)
                net_v[pl.ds(pl.multiple_of(l * 8, 8), 8), :] = jnp.sum(net.reshape(tiles, 8, columns), axis=0)
                beam_next = beam * jnp.exp2(depths[slot][l] * slant)
                diffuse = (pass_v[l] * diffuse + half * (beam - beam_next)) * inverse_v[l]
                beam = beam_next
            return beam, diffuse

        beam, diffuse = lax.fori_loop(0, steps, body, (top, jnp.zeros_like(top)))
        net_v[pl.ds(levels * 8, 8), :] = jnp.sum((beam + diffuse).reshape(tiles, 8, columns), axis=0)

    def heat_copy(j):
        return pltpu.make_async_copy(heat_v.at[j], heat_hbm.at[j], out_sem.at[j])

    def finish(j):
        at = pl.ds(levels * 8, 8)
        bottom = net_v[at, :]
        net_v[at, :] = bottom * (1.0 - state_row(j, 1))
        here = net_v[pl.ds(0, levels, stride=8), :]
        for s in range(1, 8):
            here = here + net_v[pl.ds(s, levels, stride=8), :]
        flux_v[pl.ds(0, levels), :] = here
        flux_v[pl.ds(levels, 1), :] = jnp.sum(net_v[at, :], axis=0, keepdims=True)
        below = flux_v[pl.ds(1, levels), :]
        lit = sunlit_s[(band * subs + sub) * own + j] == 1
        heating = mass_v[j].astype(jnp.float32) * (here - below)
        heat_v[j] = jnp.where(lit, heating, jnp.zeros_like(heating))
        heat_copy(j).start()
        surface_down = jnp.sum(bottom, axis=0, keepdims=True)
        surf_v[pl.ds(j, 1), :] = jnp.where(lit, surface_down, jnp.zeros_like(surface_down))

    lax.fori_loop(0, steps, lambda i, c: (optical(0, 0, i), c)[1], 0)

    def pair(p, carry):
        for slot in range(2):
            j = p * 2 + slot
            upward(j, slot)
            gas_copy(j + 1).wait()
            downward(j, slot, j + 1)
            finish(j)
        return carry

    lax.fori_loop(0, own // 2 - 1, pair, 0)
    for slot in range(2):
        j = own - 2 + slot
        upward(j, slot)
        if slot == 0:
            gas_copy(j + 1).wait()
        downward(j, slot, None if slot else j + 1)
        finish(j)
    surf_copy = pltpu.make_async_copy(surf_v, surf_hbm, in_sem.at[0])
    surf_copy.start()
    for j in range(own):
        heat_copy(j).wait()
    surf_copy.wait()


def body(gas_amounts, layer_mass, column_state, absorption, single_scatter, solar_weight, sunlit):
    subs = lax.axis_size("sub")
    blocks, levels, gases, columns = gas_amounts.shape
    share = absorption.shape[0]
    own, gpoints = blocks // subs, share * subs
    anywhere = pl.BlockSpec(memory_space=pl.ANY)
    per_level = pltpu.VMEM((levels, gpoints, columns), jnp.float32)
    net = pltpu.VMEM(((levels + 1) * 8, columns), jnp.float32)
    return pl.pallas_call(
        functools.partial(kernel, own, levels, gases, columns, gpoints, subs),
        out_shape=(
            jax.ShapeDtypeStruct((own, levels, columns), jnp.float32),
            jax.ShapeDtypeStruct((own, columns), jnp.float32),
        ),
        in_specs=[anywhere] * 7,
        out_specs=[anywhere] * 2,
        scratch_shapes=[
            pltpu.SMEM((sunlit.shape[0],), jnp.int32),
            pltpu.VMEM((own, levels * gases, columns), jnp.bfloat16),
            pltpu.VMEM((own, levels, columns), jnp.bfloat16),
            pltpu.VMEM((own, 2, columns), jnp.bfloat16),
            pltpu.VMEM((subs, gases, share), jnp.bfloat16),
            pltpu.VMEM((subs, 1, share), jnp.float32),
            pltpu.VMEM((subs, 1, share), jnp.float32),
            pltpu.VMEM((16, 128), jnp.float32),
            pltpu.VMEM((gpoints, columns), jnp.float32),
            pltpu.VMEM((gpoints, columns), jnp.float32),
            pltpu.VMEM((CHUNK * gpoints, 3 * CHUNK * gases), jnp.float32),
            pltpu.VMEM((CHUNK * gpoints, 3 * CHUNK * gases), jnp.bfloat16),
        ]
        + [per_level] * 5
        + [
            net,
            pltpu.VMEM((levels + 8, columns), jnp.float32),
            pltpu.VMEM((own, levels, columns), jnp.float32),
            pltpu.VMEM((own, columns), jnp.float32),
            pltpu.SemaphoreType.DMA((own,)),
            pltpu.SemaphoreType.DMA((6,)),
            pltpu.SemaphoreType.DMA((own,)),
            pltpu.SemaphoreType.DMA((subs, 3)),
            pltpu.SemaphoreType.DMA((subs, 3)),
        ],
        compiler_params=pltpu.CompilerParams(
            collective_id=0, has_side_effects=True, vmem_limit_bytes=60 * 1024 * 1024
        ),
        name="solve_blocks",
    )(
        gas_amounts.reshape(blocks, levels * gases, columns),
        layer_mass,
        column_state,
        absorption.T,
        single_scatter.reshape(1, share),
        solar_weight.reshape(1, share),
        sunlit,
    )


def solution(mesh):
    in_specs = (
        P("band", None, None, None),
        P("band", None, None),
        P("band", None, None),
        P("sub", None),
        P("sub"),
        P("sub"),
        P(),
    )
    out_specs = (P(("band", "sub"), None, None), P(("band", "sub"), None))
    return jax.shard_map(body, mesh=mesh, in_specs=in_specs, out_specs=out_specs, check_vma=False)
```

time: 59.9 us -> 44.6 us (0.74)
  Pallas kernels: 52.6 us -> 40.8 us
  local copies, waits for them, and re-layouts: 6.13 us -> 2.95 us
    pallas_call x2 -> x1, Pallas kernels: 52.6 us -> 40.8 us  [body(): pl.pallas_call(functools.partial(kernel, own, levels, gases, columns, gpo...]
    unnamed x13 -> x2, local copies, waits for them, and re-layouts: 6.13 us -> 2.95 us
where the time goes in v2:
time: 44.6 us; the launch traced here: 44.4 us
  Pallas kernels  40.8 us (91%)
  local copies, waits for them, and re-layouts  2.95 us (7%)
  between operations  0.64 us (1%)
    pallas_call x1, Pallas kernels, body(): pl.pallas_call(functools.partial(kernel, own, levels, gases, columns, gpo...  40.8 us
    unnamed x2, local copies, waits for them, and re-layouts  2.95 us

profile of v2, /device:TPU:1, one launch (start us, length us, event | category | flops | bytes accessed | tf_op | source)
XLA Modules:
  0.0 44.4 jit_solution(13974686797090160973)
XLA Ops:
  0.6 40.8 %solve_blocks.1 = (f32[8,64,128]{2,1,0:T(8,128)}, f32[8,128]{1,0:T(8,128)}) custom-call(bf16[64,512,128]{2,1,0:T(8,128)(2,1)} %bitcast.4, bf16[64,64,128]{2,1,0:T(8,128)(2,1)} %mass_hbm.1, bf16[64,2,128]{2,1,0:T(2,128)(2,1)} %state_hbm.1, bf16[8,14]{1,0:T(8,128)(2,1)} %bitcast.5, f32[1,14]{1,0:T(1,128)} %bitcast.6, f32[1,14]{1,0:T(1,128)} %bitcast.7, ...), custom_call_target="tpu_custom_call" | custom-call | tf_op jit(solution)/shard_map/solve_blocks/pallas_call | solution.py:211
  41.5 1.7 %copy.11 = f32[8,64,128]{2,1,0:T(8,128)} copy(f32[8,64,128]{2,1,0:T(8,128)} %get-tuple-element.4) | data formatting | bytes 524288
  43.1 1.3 %copy.12 = f32[8,128]{1,0:T(8,128)} copy(f32[8,128]{1,0:T(8,128)} %get-tuple-element.5) | data formatting | bytes 8192

commit v3 on v2

v3 whole, which is shorter than its diff:
```python
import functools
import math

import jax
import jax.numpy as jnp
from jax import lax
from jax.experimental import pallas as pl
from jax.experimental.pallas import tpu as pltpu
from jax.sharding import PartitionSpec as P

MESH = pl.DeviceIdType.MESH
LOG2E = math.log2(math.e)
CHUNK = 8
STEP = 32
GROUPS = 2


def exchange_kernel(gases, share, subs, table_hbm, omega_hbm, weight_hbm, packed_hbm, table_v, omega_v, weight_v, pack_v, in_sem, send_sem, recv_sem):
    band = lax.axis_index("band")
    sub = lax.axis_index("sub")
    barrier = pltpu.get_barrier_semaphore()
    for step in range(1, subs):
        pl.semaphore_signal(barrier, inc=1, device_id=(band, lax.rem(sub + step, subs)), device_id_type=MESH)
    tables = ((table_hbm, table_v), (omega_hbm, omega_v), (weight_hbm, weight_v))
    copies = [pltpu.make_async_copy(source, target, in_sem.at[k]) for k, (source, target) in enumerate(tables)]
    for copy in copies:
        copy.start()
    for copy in copies:
        copy.wait()
    pack_v[0:gases, 0:share] = table_v[...].astype(jnp.float32)
    pack_v[0:1, 32 : 32 + share] = omega_v[...]
    pack_v[0:1, 64 : 64 + share] = weight_v[...]
    pl.semaphore_wait(barrier, subs - 1)
    sent = []
    for step in range(1, subs):
        copy = pltpu.make_async_remote_copy(
            src_ref=pack_v,
            dst_ref=packed_hbm.at[sub],
            send_sem=send_sem.at[step],
            recv_sem=recv_sem.at[step],
            device_id=(band, lax.rem(sub + step, subs)),
            device_id_type=MESH,
        )
        copy.start()
        sent.append(copy)
    own_part = pltpu.make_async_copy(pack_v, packed_hbm.at[sub], in_sem.at[0])
    own_part.start()
    own_part.wait()
    for copy in sent:
        copy.wait()


def exchange(absorption, single_scatter, solar_weight, subs):
    share, gases = absorption.shape
    anywhere = pl.BlockSpec(memory_space=pl.ANY)
    return pl.pallas_call(
        functools.partial(exchange_kernel, gases, share, subs),
        out_shape=jax.ShapeDtypeStruct((subs, 8, 128), jnp.float32),
        in_specs=[anywhere] * 3,
        out_specs=anywhere,
        scratch_shapes=[
            pltpu.VMEM((gases, share), jnp.bfloat16),
            pltpu.VMEM((1, share), jnp.float32),
            pltpu.VMEM((1, share), jnp.float32),
            pltpu.VMEM((8, 128), jnp.float32),
            pltpu.SemaphoreType.DMA((3,)),
            pltpu.SemaphoreType.DMA((subs,)),
            pltpu.SemaphoreType.DMA((subs,)),
        ],
        compiler_params=pltpu.CompilerParams(collective_id=0, has_side_effects=True),
        name="exchange_tables",
    )(absorption.T, single_scatter.reshape(1, share), solar_weight.reshape(1, share))


def kernel(
    own, levels, gases, columns, gpoints, subs,
    gas_hbm, mass_hbm, state_hbm, packed_hbm, sunlit_hbm,
    heat_hbm, surf_hbm,
    sunlit_s, gas_v, mass_v, state_v, pack_v, lay_v, half_v, top_v, spread_v, coef_v,
    depth_00, depth_01, depth_10, depth_11, pass_0, pass_1, upper_0, upper_1, lower_0, lower_1, net_0, net_v, flux_v, heat_v, surf_v,
    gas_sem, in_sem, out_sem,
):
    band = lax.axis_index("band")
    sub = lax.axis_index("sub")
    share = gpoints // subs
    rows = gpoints // GROUPS
    tiles = rows // 8
    steps = levels // STEP
    dots = STEP // CHUNK
    width = CHUNK * gases
    first = sub * own

    packed_copy = pltpu.make_async_copy(packed_hbm, pack_v, in_sem.at[1])
    packed_copy.start()

    def gas_copy(j):
        return pltpu.make_async_copy(gas_hbm.at[first + j], gas_v.at[j], gas_sem.at[j])

    others = [
        pltpu.make_async_copy(state_hbm.at[pl.ds(first, own)], state_v, in_sem.at[3]),
        pltpu.make_async_copy(mass_hbm.at[pl.ds(first, own)], mass_v, in_sem.at[4]),
        pltpu.make_async_copy(sunlit_hbm, sunlit_s, in_sem.at[5]),
    ]
    for j in range(own):
        gas_copy(j).start()
    for copy in others:
        copy.start()
    lay_v[...] = jnp.zeros_like(lay_v)
    spread_v[...] = jnp.zeros_like(spread_v)
    packed_copy.wait()
    for copy in others:
        copy.wait()
    gas_copy(0).wait()

    for s in range(subs):
        at = slice(s * share, (s + 1) * share)
        lay_v[0:gases, at] = pack_v[s, 0:gases, 0:share]
        lay_v[gases : gases + 1, at] = pack_v[s, 0:1, 32 : 32 + share]
        lay_v[gases + 1 : gases + 2, at] = pack_v[s, 0:1, 64 : 64 + share]
    by_row = jnp.transpose(lay_v[...])[:gpoints]
    coef = by_row[:, :gases] * (-LOG2E)
    half_v[...] = jnp.broadcast_to(0.5 * by_row[:, gases : gases + 1], (gpoints, columns))
    top_v[...] = jnp.broadcast_to(by_row[:, gases + 1 : gases + 2], (gpoints, columns))
    high = coef.astype(jnp.bfloat16).astype(jnp.float32)
    middle = (coef - high).astype(jnp.bfloat16).astype(jnp.float32)
    low = coef - high - middle
    for k, part in enumerate((high, middle, low)):
        for g in range(GROUPS):
            for l in range(CHUNK):
                at = k * width + l * gases
                spread_v[pl.ds((g * CHUNK + l) * rows, rows), at : at + gases] = part[g * rows : (g + 1) * rows]
    coef_v[...] = spread_v[...].astype(jnp.bfloat16)

    depths = ((depth_00, depth_01), (depth_10, depth_11))
    passes, uppers, lowers, nets = (pass_0, pass_1), (upper_0, upper_1), (lower_0, lower_1), (net_0, net_v)

    def state_row(j, k):
        row = state_v[j].astype(jnp.float32)[k : k + 1, :]
        return jnp.broadcast_to(row, (8, columns))

    def all_rows(row):
        return jnp.broadcast_to(row[None], (tiles, 8, columns)).reshape(rows, columns)

    def optical(j, slot, g, i):
        amounts = jnp.concatenate(
            [gas_v[j, pl.ds(pl.multiple_of((i * dots + d) * width, width), width), :] for d in range(dots)], axis=1
        )
        amounts = jnp.concatenate([amounts] * 3, axis=0)
        return jnp.dot(coef_v[pl.ds(g * CHUNK * rows, CHUNK * rows), :], amounts, preferred_element_type=jnp.float32)

    def keep(depth, slot, g, i):
        for d in range(dots):
            for m in range(CHUNK):
                part = depth[m * rows : (m + 1) * rows, d * columns : (d + 1) * columns]
                depths[slot][g][i * STEP + d * CHUNK + m] = part

    def run(down, up, coming):
        start = ()
        if up is not None:
            ground = all_rows(state_row(up[0], 1))
            start += (ground, jnp.ones_like(ground))
        if down is not None:
            mu = all_rows(state_row(down[0], 0))
            slant = 1.0 / mu
            top = top_v[pl.ds(down[2] * rows, rows), :] * mu
            start += (top, jnp.zeros_like(top))

        def body(i, carry):
            carry = list(carry)
            if coming is not None:
                ready = optical(*coming, i)
            if up is not None:
                _, slot, g = up
                upper, lower = carry[:2]
                half_up = half_v[pl.ds(g * rows, rows), :]
            if down is not None:
                _, slot_d, g_d = down
                beam, scaled = carry[-2:]
                half_down = half_v[pl.ds(g_d * rows, rows), :]
            for k in range(STEP):
                if up is not None:
                    l = levels - 1 - (i * STEP + k)
                    passing = jnp.exp2(depths[slot][g][l])
                    passes[g][l] = passing
                    square = passing * passing
                    reflected = half_up - half_up * square
                    lower = lower - reflected * upper
                    upper = reflected * lower + square * upper
                    uppers[g][l] = upper
                    lowers[g][l] = lower
                if down is not None:
                    l = i * STEP + k
                    below = lowers[g_d][l]
                    inverse = 1.0 / below
                    net = (below - uppers[g_d][l]) * (beam * inverse + scaled)
                    at = pl.ds(pl.multiple_of(l * 8, 8), 8)
                    net = jnp.sum(net.reshape(tiles, 8, columns), axis=0)
                    nets[g_d][at, :] = net if g_d == 0 else net + nets[0][at, :]
                    beam_next = beam * jnp.exp2(depths[slot_d][g_d][l] * slant)
                    scaled = passes[g_d][l] * scaled + (half_down * (beam - beam_next)) * inverse
                    beam = beam_next
            if coming is not None:
                keep(ready, *coming[1:], i)
            return (() if up is None else (upper, lower)) + (() if down is None else (beam, scaled))

        end = lax.fori_loop(0, steps, body, start)
        if down is not None:
            beam, diffuse = end[-2:]
            at = pl.ds(levels * 8, 8)
            net = jnp.sum((beam + diffuse).reshape(tiles, 8, columns), axis=0)
            nets[down[2]][at, :] = net if down[2] == 0 else net + nets[0][at, :]

    def heat_copy(j):
        return pltpu.make_async_copy(heat_v.at[j], heat_hbm.at[j], out_sem.at[j])

    def finish(j):
        at = pl.ds(levels * 8, 8)
        bottom = net_v[at, :]
        net_v[at, :] = bottom * (1.0 - state_row(j, 1))
        here = net_v[pl.ds(0, levels, stride=8), :]
        for s in range(1, 8):
            here = here + net_v[pl.ds(s, levels, stride=8), :]
        flux_v[pl.ds(0, levels), :] = here
        flux_v[pl.ds(levels, 1), :] = jnp.sum(net_v[at, :], axis=0, keepdims=True)
        below = flux_v[pl.ds(1, levels), :]
        lit = sunlit_s[(band * subs + sub) * own + j] == 1
        heating = mass_v[j].astype(jnp.float32) * (here - below)
        heat_v[j] = jnp.where(lit, heating, jnp.zeros_like(heating))
        heat_copy(j).start()
        surface_down = jnp.sum(bottom, axis=0, keepdims=True)
        surf_v[pl.ds(j, 1), :] = jnp.where(lit, surface_down, jnp.zeros_like(surface_down))

    def prepare(i, carry):
        for g in range(GROUPS):
            keep(optical(0, 0, g, i), 0, g, i)
        return carry

    lax.fori_loop(0, steps, prepare, 0)
    run(None, (0, 0, 0), None)

    def pair(p, carry):
        for slot in range(2):
            j = p * 2 + slot
            other = 1 - slot
            gas_copy(j + 1).wait()
            run((j, slot, 0), (j, slot, 1), (j + 1, other, 0))
            run((j, slot, 1), (j + 1, other, 0), (j + 1, other, 1))
            finish(j)
        return carry

    lax.fori_loop(0, own // 2 - 1, pair, 0)
    j = own - 2
    gas_copy(j + 1).wait()
    run((j, 0, 0), (j, 0, 1), (j + 1, 1, 0))
    run((j, 0, 1), (j + 1, 1, 0), (j + 1, 1, 1))
    finish(j)
    run((j + 1, 1, 0), (j + 1, 1, 1), None)
    run((j + 1, 1, 1), None, None)
    finish(j + 1)
    surf_copy = pltpu.make_async_copy(surf_v, surf_hbm, in_sem.at[0])
    surf_copy.start()
    for j in range(own):
        heat_copy(j).wait()
    surf_copy.wait()


def body(gas_amounts, layer_mass, column_state, absorption, single_scatter, solar_weight, sunlit):
    subs = lax.axis_size("sub")
    blocks, levels, gases, columns = gas_amounts.shape
    share = absorption.shape[0]
    own, gpoints = blocks // subs, share * subs
    anywhere = pl.BlockSpec(memory_space=pl.ANY)
    per_level = pltpu.VMEM((levels, gpoints // GROUPS, columns), jnp.float32)
    net = pltpu.VMEM(((levels + 1) * 8, columns), jnp.float32)
    return pl.pallas_call(
        functools.partial(kernel, own, levels, gases, columns, gpoints, subs),
        out_shape=(
            jax.ShapeDtypeStruct((own, levels, columns), jnp.float32),
            jax.ShapeDtypeStruct((own, columns), jnp.float32),
        ),
        in_specs=[anywhere] * 5,
        out_specs=[anywhere] * 2,
        scratch_shapes=[
            pltpu.SMEM((sunlit.shape[0],), jnp.int32),
            pltpu.VMEM((own, levels * gases, columns), jnp.bfloat16),
            pltpu.VMEM((own, levels, columns), jnp.bfloat16),
            pltpu.VMEM((own, 2, columns), jnp.bfloat16),
            pltpu.VMEM((subs, 8, 128), jnp.float32),
            pltpu.VMEM((16, 128), jnp.float32),
            pltpu.VMEM((gpoints, columns), jnp.float32),
            pltpu.VMEM((gpoints, columns), jnp.float32),
            pltpu.VMEM((CHUNK * gpoints, 3 * CHUNK * gases), jnp.float32),
            pltpu.VMEM((CHUNK * gpoints, 3 * CHUNK * gases), jnp.bfloat16),
        ]
        + [per_level] * 10
        + [
            net, net,
            pltpu.VMEM((levels + 8, columns), jnp.float32),
            pltpu.VMEM((own, levels, columns), jnp.float32),
            pltpu.VMEM((own, columns), jnp.float32),
            pltpu.SemaphoreType.DMA((own,)),
            pltpu.SemaphoreType.DMA((6,)),
            pltpu.SemaphoreType.DMA((own,)),
        ],
        compiler_params=pltpu.CompilerParams(
            vmem_limit_bytes=60 * 1024 * 1024
        ),
        name="solve_blocks",
    )(
        gas_amounts.reshape(blocks, levels * gases, columns),
        layer_mass,
        column_state,
        exchange(absorption, single_scatter, solar_weight, subs),
        sunlit,
    )


def solution(mesh):
    in_specs = (
        P("band", None, None, None),
        P("band", None, None),
        P("band", None, None),
        P("sub", None),
        P("sub"),
        P("sub"),
        P(),
    )
    out_specs = (P(("band", "sub"), None, None), P(("band", "sub"), None))
    return jax.shard_map(body, mesh=mesh, in_specs=in_specs, out_specs=out_specs, check_vma=False)
```

time: 44.6 us -> 39.3 us (0.88)
  local copies, waits for them, and re-layouts: 2.95 us -> 0 us
  Pallas kernels: 40.8 us -> 38.5 us
    pallas_call x1, Pallas kernels: 40.8 us -> 29.9 us  [body(): pl.pallas_call(functools.partial(kernel, own, levels, gases, columns, gpo...]
    pallas_call x0 -> x1, Pallas kernels: none -> 8.68 us  [exchange(): pl.pallas_call(functools.partial(exchange_kernel, gases, share, subs), ou...]
    unnamed x2 -> x0, local copies, waits for them, and re-layouts: 2.95 us -> none
where the time goes in v3:
time: 39.3 us; the launch traced here: 39.2 us
  Pallas kernels  38.5 us (98%)
  between operations  0.64 us (2%)
    pallas_call x1, Pallas kernels, body(): pl.pallas_call(functools.partial(kernel, own, levels, gases, columns, gpo...  29.9 us
    pallas_call x1, Pallas kernels, exchange(): pl.pallas_call(functools.partial(exchange_kernel, gases, share, subs), ou...  8.68 us

profile of v3, /device:TPU:1, one launch (start us, length us, event | category | flops | bytes accessed | tf_op | source)
XLA Modules:
  0.0 39.2 jit_solution(11462788870186437771)
XLA Ops:
  0.6 8.7 %exchange_tables.1.packed_hbm = f32[8,8,128]{2,1,0:T(8,128)} custom-call(bf16[8,14]{1,0:T(8,128)(2,1)} %bitcast.5, f32[1,14]{1,0:T(1,128)} %bitcast.6, f32[1,14]{1,0:T(1,128)} %bitcast.7), custom_call_target="tpu_custom_call" | custom-call | tf_op jit(solution)/shard_map/exchange_tables/pallas_call | solution.py:56
  9.3 29.9 %solve_blocks.1 = (f32[8,64,128]{2,1,0:T(8,128)}, f32[8,128]{1,0:T(8,128)}) custom-call(bf16[64,512,128]{2,1,0:T(8,128)(2,1)} %bitcast.4, bf16[64,64,128]{2,1,0:T(8,128)(2,1)} %mass_hbm.1, bf16[64,2,128]{2,1,0:T(2,128)(2,1)} %state_hbm.1, f32[8,8,128]{2,1,0:T(8,128)} %exchange_tables.1.packed_hbm, s32[1024]{0:T(1024)} %sunlit_hbm.1), custom_call_target="tpu_custom_call" | custom-call | tf_op jit(solution)/shard_map/solve_blocks/pallas_call | solution.py:275

commit v4 on v3

--- a/solution.py
+++ b/solution.py
@@ -15,27 +15,42 @@
 GROUPS = 2
 
 
-def exchange_kernel(gases, share, subs, table_hbm, omega_hbm, weight_hbm, packed_hbm, table_v, omega_v, weight_v, pack_v, in_sem, send_sem, recv_sem):
+def exchange_kernel(
+    own, levels, gases, columns, share, subs,
+    gas_hbm, mass_hbm, state_hbm, table_hbm, omega_hbm, weight_hbm,
+    gas_out, mass_out, state_out, coef_out, half_out, top_out,
+    table_v, omega_v, weight_v, pack_v, lay_v, spread_v, in_sem, send_sem, recv_sem,
+):
     band = lax.axis_index("band")
     sub = lax.axis_index("sub")
+    gpoints = share * subs
+    rows = gpoints // GROUPS
+    width = CHUNK * gases
     barrier = pltpu.get_barrier_semaphore()
     for step in range(1, subs):
         pl.semaphore_signal(barrier, inc=1, device_id=(band, lax.rem(sub + step, subs)), device_id_type=MESH)
     tables = ((table_hbm, table_v), (omega_hbm, omega_v), (weight_hbm, weight_v))
     copies = [pltpu.make_async_copy(source, target, in_sem.at[k]) for k, (source, target) in enumerate(tables)]
-    for copy in copies:
+    blocks = ((gas_hbm, gas_out), (mass_hbm, mass_out), (state_hbm, state_out))
+    others = [
+        pltpu.make_async_copy(source.at[pl.ds(sub * own, own)], target, in_sem.at[3 + k])
+        for k, (source, target) in enumerate(blocks)
+    ]
+    for copy in copies + others:
         copy.start()
+    lay_v[...] = jnp.zeros_like(lay_v)
+    spread_v[...] = jnp.zeros_like(spread_v)
     for copy in copies:
         copy.wait()
-    pack_v[0:gases, 0:share] = table_v[...].astype(jnp.float32)
-    pack_v[0:1, 32 : 32 + share] = omega_v[...]
-    pack_v[0:1, 64 : 64 + share] = weight_v[...]
+    pack_v[sub, 0:gases, 0:share] = table_v[...].astype(jnp.float32)
+    pack_v[sub, 0:1, 32 : 32 + share] = omega_v[...]
+    pack_v[sub, 0:1, 64 : 64 + share] = weight_v[...]
     pl.semaphore_wait(barrier, subs - 1)
     sent = []
     for step in range(1, subs):
         copy = pltpu.make_async_remote_copy(
-            src_ref=pack_v,
-            dst_ref=packed_hbm.at[sub],
+            src_ref=pack_v.at[sub],
+            dst_ref=pack_v.at[sub],
             send_sem=send_sem.at[step],
             recv_sem=recv_sem.at[step],
             device_id=(band, lax.rem(sub + step, subs)),
@@ -43,74 +58,10 @@
         )
         copy.start()
         sent.append(copy)
-    own_part = pltpu.make_async_copy(pack_v, packed_hbm.at[sub], in_sem.at[0])
-    own_part.start()
-    own_part.wait()
+    for copy in others:
+        copy.wait()
     for copy in sent:
         copy.wait()
-
-
-def exchange(absorption, single_scatter, solar_weight, subs):
-    share, gases = absorption.shape
-    anywhere = pl.BlockSpec(memory_space=pl.ANY)
-    return pl.pallas_call(
-        functools.partial(exchange_kernel, gases, share, subs),
-        out_shape=jax.ShapeDtypeStruct((subs, 8, 128), jnp.float32),
-        in_specs=[anywhere] * 3,
-        out_specs=anywhere,
-        scratch_shapes=[
-            pltpu.VMEM((gases, share), jnp.bfloat16),
-            pltpu.VMEM((1, share), jnp.float32),
-            pltpu.VMEM((1, share), jnp.float32),
-            pltpu.VMEM((8, 128), jnp.float32),
-            pltpu.SemaphoreType.DMA((3,)),
-            pltpu.SemaphoreType.DMA((subs,)),
-            pltpu.SemaphoreType.DMA((subs,)),
-        ],
-        compiler_params=pltpu.CompilerParams(collective_id=0, has_side_effects=True),
-        name="exchange_tables",
-    )(absorption.T, single_scatter.reshape(1, share), solar_weight.reshape(1, share))
-
-
-def kernel(
-    own, levels, gases, columns, gpoints, subs,
-    gas_hbm, mass_hbm, state_hbm, packed_hbm, sunlit_hbm,
-    heat_hbm, surf_hbm,
-    sunlit_s, gas_v, mass_v, state_v, pack_v, lay_v, half_v, top_v, spread_v, coef_v,
-    depth_00, depth_01, depth_10, depth_11, pass_0, pass_1, upper_0, upper_1, lower_0, lower_1, net_0, net_v, flux_v, heat_v, surf_v,
-    gas_sem, in_sem, out_sem,
-):
-    band = lax.axis_index("band")
-    sub = lax.axis_index("sub")
-    share = gpoints // subs
-    rows = gpoints // GROUPS
-    tiles = rows // 8
-    steps = levels // STEP
-    dots = STEP // CHUNK
-    width = CHUNK * gases
-    first = sub * own
-
-    packed_copy = pltpu.make_async_copy(packed_hbm, pack_v, in_sem.at[1])
-    packed_copy.start()
-
-    def gas_copy(j):
-        return pltpu.make_async_copy(gas_hbm.at[first + j], gas_v.at[j], gas_sem.at[j])
-
-    others = [
-        pltpu.make_async_copy(state_hbm.at[pl.ds(first, own)], state_v, in_sem.at[3]),
-        pltpu.make_async_copy(mass_hbm.at[pl.ds(first, own)], mass_v, in_sem.at[4]),
-        pltpu.make_async_copy(sunlit_hbm, sunlit_s, in_sem.at[5]),
-    ]
-    for j in range(own):
-        gas_copy(j).start()
-    for copy in others:
-        copy.start()
-    lay_v[...] = jnp.zeros_like(lay_v)
-    spread_v[...] = jnp.zeros_like(spread_v)
-    packed_copy.wait()
-    for copy in others:
-        copy.wait()
-    gas_copy(0).wait()
 
     for s in range(subs):
         at = slice(s * share, (s + 1) * share)
@@ -119,8 +70,8 @@
         lay_v[gases + 1 : gases + 2, at] = pack_v[s, 0:1, 64 : 64 + share]
     by_row = jnp.transpose(lay_v[...])[:gpoints]
     coef = by_row[:, :gases] * (-LOG2E)
-    half_v[...] = jnp.broadcast_to(0.5 * by_row[:, gases : gases + 1], (gpoints, columns))
-    top_v[...] = jnp.broadcast_to(by_row[:, gases + 1 : gases + 2], (gpoints, columns))
+    half_out[...] = jnp.broadcast_to(0.5 * by_row[:, gases : gases + 1], (gpoints, columns))
+    top_out[...] = jnp.broadcast_to(by_row[:, gases + 1 : gases + 2], (gpoints, columns))
     high = coef.astype(jnp.bfloat16).astype(jnp.float32)
     middle = (coef - high).astype(jnp.bfloat16).astype(jnp.float32)
     low = coef - high - middle
@@ -129,7 +80,62 @@
             for l in range(CHUNK):
                 at = k * width + l * gases
                 spread_v[pl.ds((g * CHUNK + l) * rows, rows), at : at + gases] = part[g * rows : (g + 1) * rows]
-    coef_v[...] = spread_v[...].astype(jnp.bfloat16)
+    coef_out[...] = spread_v[...].astype(jnp.bfloat16)
+
+
+def exchange(gas, layer_mass, column_state, absorption, single_scatter, solar_weight, subs):
+    share, gases = absorption.shape
+    blocks, depth, columns = gas.shape
+    own, levels, gpoints = blocks // subs, depth // gases, share * subs
+    anywhere = pl.BlockSpec(memory_space=pltpu.HBM)
+    vmem = pl.BlockSpec(memory_space=pltpu.VMEM)
+    return pl.pallas_call(
+        functools.partial(exchange_kernel, own, levels, gases, columns, share, subs),
+        out_shape=(
+            pltpu.VMEM((own, depth, columns), jnp.bfloat16),
+            pltpu.VMEM((own, levels, columns), jnp.bfloat16),
+            pltpu.VMEM((own, 2, columns), jnp.bfloat16),
+            pltpu.VMEM((CHUNK * gpoints, 3 * CHUNK * gases), jnp.bfloat16),
+            pltpu.VMEM((gpoints, columns), jnp.float32),
+            pltpu.VMEM((gpoints, columns), jnp.float32),
+        ),
+        in_specs=[anywhere] * 6,
+        out_specs=[vmem] * 6,
+        scratch_shapes=[
+            pltpu.VMEM((gases, share), jnp.bfloat16),
+            pltpu.VMEM((1, share), jnp.float32),
+            pltpu.VMEM((1, share), jnp.float32),
+            pltpu.VMEM((subs, 8, 128), jnp.float32),
+            pltpu.VMEM((16, 128), jnp.float32),
+            pltpu.VMEM((CHUNK * gpoints, 3 * CHUNK * gases), jnp.float32),
+            pltpu.SemaphoreType.DMA((6,)),
+            pltpu.SemaphoreType.DMA((subs,)),
+            pltpu.SemaphoreType.DMA((subs,)),
+        ],
+        compiler_params=pltpu.CompilerParams(
+            collective_id=0, has_side_effects=True, vmem_limit_bytes=65100000
+        ),
+        name="exchange_tables",
+    )(gas, layer_mass, column_state, absorption.T, single_scatter.reshape(1, share), solar_weight.reshape(1, share))
+
+
+def kernel(
+    own, levels, gases, columns, gpoints, subs,
+    gas_v, mass_v, state_v, coef_v, half_v, top_v, sunlit_hbm,
+    heat_hbm, surf_hbm,
+    sunlit_s, depth_00, depth_01, depth_10, depth_11, pass_0, pass_1, upper_0, upper_1, lower_0, lower_1, net_0, net_v, flux_v, heat_v, surf_v,
+    in_sem, out_sem,
+):
+    band = lax.axis_index("band")
+    sub = lax.axis_index("sub")
+    rows = gpoints // GROUPS
+    tiles = rows // 8
+    steps = levels // STEP
+    dots = STEP // CHUNK
+    width = CHUNK * gases
+
+    lit_copy = pltpu.make_async_copy(sunlit_hbm, sunlit_s, in_sem.at[0])
+    lit_copy.start()
 
     depths = ((depth_00, depth_01), (depth_10, depth_11))
     passes, uppers, lowers, nets = (pass_0, pass_1), (upper_0, upper_1), (lower_0, lower_1), (net_0, net_v)
@@ -231,18 +237,17 @@
         surf_v[pl.ds(j, 1), :] = jnp.where(lit, surface_down, jnp.zeros_like(surface_down))
 
     def prepare(i, carry):
-        for g in range(GROUPS):
-            keep(optical(0, 0, g, i), 0, g, i)
+        keep(optical(0, 0, 0, i), 0, 0, i)
         return carry
 
     lax.fori_loop(0, steps, prepare, 0)
-    run(None, (0, 0, 0), None)
+    run(None, (0, 0, 0), (0, 0, 1))
+    lit_copy.wait()
 
     def pair(p, carry):
         for slot in range(2):
             j = p * 2 + slot
             other = 1 - slot
-            gas_copy(j + 1).wait()
             run((j, slot, 0), (j, slot, 1), (j + 1, other, 0))
             run((j, slot, 1), (j + 1, other, 0), (j + 1, other, 1))
             finish(j)
@@ -250,14 +255,13 @@
 
     lax.fori_loop(0, own // 2 - 1, pair, 0)
     j = own - 2
-    gas_copy(j + 1).wait()
     run((j, 0, 0), (j, 0, 1), (j + 1, 1, 0))
     run((j, 0, 1), (j + 1, 1, 0), (j + 1, 1, 1))
     finish(j)
     run((j + 1, 1, 0), (j + 1, 1, 1), None)
     run((j + 1, 1, 1), None, None)
     finish(j + 1)
-    surf_copy = pltpu.make_async_copy(surf_v, surf_hbm, in_sem.at[0])
+    surf_copy = pltpu.make_async_copy(surf_v, surf_hbm, in_sem.at[1])
     surf_copy.start()
     for j in range(own):
         heat_copy(j).wait()
@@ -269,7 +273,7 @@
     blocks, levels, gases, columns = gas_amounts.shape
     share = absorption.shape[0]
     own, gpoints = blocks // subs, share * subs
-    anywhere = pl.BlockSpec(memory_space=pl.ANY)
+    anywhere = pl.BlockSpec(memory_space=pltpu.HBM)
     per_level = pltpu.VMEM((levels, gpoints // GROUPS, columns), jnp.float32)
     net = pltpu.VMEM(((levels + 1) * 8, columns), jnp.float32)
     return pl.pallas_call(
@@ -278,19 +282,10 @@
             jax.ShapeDtypeStruct((own, levels, columns), jnp.float32),
             jax.ShapeDtypeStruct((own, columns), jnp.float32),
         ),
-        in_specs=[anywhere] * 5,
+        in_specs=[pl.BlockSpec(memory_space=pltpu.VMEM)] * 6 + [anywhere],
         out_specs=[anywhere] * 2,
         scratch_shapes=[
             pltpu.SMEM((sunlit.shape[0],), jnp.int32),
-            pltpu.VMEM((own, levels * gases, columns), jnp.bfloat16),
-            pltpu.VMEM((own, levels, columns), jnp.bfloat16),
-            pltpu.VMEM((own, 2, columns), jnp.bfloat16),
-            pltpu.VMEM((subs, 8, 128), jnp.float32),
-            pltpu.VMEM((16, 128), jnp.float32),
-            pltpu.VMEM((gpoints, columns), jnp.float32),
-            pltpu.VMEM((gpoints, columns), jnp.float32),
-            pltpu.VMEM((CHUNK * gpoints, 3 * CHUNK * gases), jnp.float32),
-            pltpu.VMEM((CHUNK * gpoints, 3 * CHUNK * gases), jnp.bfloat16),
         ]
         + [per_level] * 10
         + [
@@ -298,19 +293,23 @@
             pltpu.VMEM((levels + 8, columns), jnp.float32),
             pltpu.VMEM((own, levels, columns), jnp.float32),
             pltpu.VMEM((own, columns), jnp.float32),
-            pltpu.SemaphoreType.DMA((own,)),
-            pltpu.SemaphoreType.DMA((6,)),
+            pltpu.SemaphoreType.DMA((2,)),
             pltpu.SemaphoreType.DMA((own,)),
         ],
         compiler_params=pltpu.CompilerParams(
-            vmem_limit_bytes=60 * 1024 * 1024
+            vmem_limit_bytes=40 * 1024 * 1024
         ),
         name="solve_blocks",
     )(
-        gas_amounts.reshape(blocks, levels * gases, columns),
-        layer_mass,
-        column_state,
-        exchange(absorption, single_scatter, solar_weight, subs),
+        *exchange(
+            gas_amounts.reshape(blocks, levels * gases, columns),
+            layer_mass,
+            column_state,
+            absorption,
+            single_scatter,
+            solar_weight,
+            subs,
+        ),
         sunlit,
     )
 

time: 39.3 us -> 37.5 us (0.954)
  Pallas kernels: 38.5 us -> 36.7 us
    pallas_call x1, Pallas kernels: 29.9 us -> 27.5 us  [body(): pl.pallas_call(functools.partial(kernel, own, levels, gases, columns, gpo...]
    pallas_call x1, Pallas kernels: 8.68 us -> 9.2 us  [exchange(): pl.pallas_call(functools.partial(exchange_kernel, own, levels, gases, col...]
where the time goes in v4:
time: 37.5 us; the launch traced here: 37.4 us
  Pallas kernels  36.7 us (98%)
  between operations  0.66 us (2%)
    pallas_call x1, Pallas kernels, body(): pl.pallas_call(functools.partial(kernel, own, levels, gases, columns, gpo...  27.5 us
    pallas_call x1, Pallas kernels, exchange(): pl.pallas_call(functools.partial(exchange_kernel, own, levels, gases, col...  9.2 us

profile of v4, /device:TPU:1, one launch (start us, length us, event | category | flops | bytes accessed | tf_op | source)
XLA Modules:
  0.0 37.4 jit_solution(1928017155274886960)
XLA Ops:
  0.6 0.0 copy-start
  0.6 9.2 %exchange_tables.1 = (bf16[8,512,128]{2,1,0:T(8,128)(2,1)S(1)}, bf16[8,64,128]{2,1,0:T(8,128)(2,1)S(1)}, bf16[8,2,128]{2,1,0:T(2,128)(2,1)S(1)}, bf16[896,192]{1...) custom-call(bf16[64,512,128]{2,1,0:T(8,128)(2,1)} %bitcast.4, bf16[64,64,128]{2,1,0:T(8,128)(2,1)} %mass_hbm.1, ...), custom_call_target="tpu_custom_call" | custom-call | tf_op jit(solution)/shard_map/exchange_tables/pallas_call | solution.py:92
  9.9 0.0 copy-done
  9.9 27.5 %solve_blocks.1 = (f32[8,64,128]{2,1,0:T(8,128)}, f32[8,128]{1,0:T(8,128)}) custom-call(bf16[8,512,128]{2,1,0:T(8,128)(2,1)S(1)} %get-tuple-element.8.gas_v, bf16[8,64,128]{2,1,0:T(8,128)(2,1)S(1)} %get-tuple-element.9.mass_v, bf16[8,2,128]{2,1,0:T(2,128)(2,1)S(1)} %get-tuple-element.10.state_v, bf16[896,192]{1,0:T(8,128)(2,1)S(1)} %get-tuple-element.11.coef_v, ...), custom_call_target="tpu_custom_call" | custom-call | tf_op jit(solution)/shard_map/solve_blocks/pallas_call | solution.py:279
Async XLA Ops:
  0.6 9.2 %copy-start = (s32[1024]{0:T(1024)S(1)}, s32[1024]{0:T(1024)}, u32[]{:S(2)}) copy-start(s32[1024]{0:T(1024)} %sunlit_hbm.1) | copy-start | bytes 12292

commit v5 on v4

--- a/solution.py
+++ b/solution.py
@@ -15,10 +15,16 @@
 GROUPS = 2
 
 
+def in_three(x):
+    high = x.astype(jnp.bfloat16).astype(jnp.float32)
+    middle = (x - high).astype(jnp.bfloat16).astype(jnp.float32)
+    return high, middle, x - high - middle
+
+
 def exchange_kernel(
     own, levels, gases, columns, share, subs,
     gas_hbm, mass_hbm, state_hbm, table_hbm, omega_hbm, weight_hbm,
-    gas_out, mass_out, state_out, coef_out, half_out, top_out,
+    gas_out, mass_out, state_out, path_out, pass_out, beam_out, half_out, top_out,
     table_v, omega_v, weight_v, pack_v, lay_v, spread_v, in_sem, send_sem, recv_sem,
 ):
     band = lax.axis_index("band")
@@ -60,6 +66,25 @@
         sent.append(copy)
     for copy in others:
         copy.wait()
+
+    slants = [
+        jnp.broadcast_to((-LOG2E) / state_out[j].astype(jnp.float32)[0:1, :], (8, columns)) for j in range(own)
+    ]
+
+    def add_layers(m, totals):
+        at = pl.ds(pl.multiple_of(m * 16, 16), 16)
+        after = []
+        for j in range(own):
+            amounts = gas_out[j, at, :].astype(jnp.float32)
+            upper = totals[j] + amounts[:8]
+            lower = upper + amounts[8:]
+            both = jnp.concatenate([upper * slants[j], lower * slants[j]], axis=0)
+            for k, term in enumerate(in_three(both)):
+                path_out[k, j, at, :] = term.astype(jnp.bfloat16)
+            after.append(lower)
+        return tuple(after)
+
+    lax.fori_loop(0, levels // 2, add_layers, tuple(jnp.zeros_like(slant) for slant in slants))
     for copy in sent:
         copy.wait()
 
@@ -69,18 +94,29 @@
         lay_v[gases : gases + 1, at] = pack_v[s, 0:1, 32 : 32 + share]
         lay_v[gases + 1 : gases + 2, at] = pack_v[s, 0:1, 64 : 64 + share]
     by_row = jnp.transpose(lay_v[...])[:gpoints]
-    coef = by_row[:, :gases] * (-LOG2E)
+    weight = by_row[:, gases + 1 : gases + 2]
     half_out[...] = jnp.broadcast_to(0.5 * by_row[:, gases : gases + 1], (gpoints, columns))
-    top_out[...] = jnp.broadcast_to(by_row[:, gases + 1 : gases + 2], (gpoints, columns))
-    high = coef.astype(jnp.bfloat16).astype(jnp.float32)
-    middle = (coef - high).astype(jnp.bfloat16).astype(jnp.float32)
-    low = coef - high - middle
-    for k, part in enumerate((high, middle, low)):
-        for g in range(GROUPS):
-            for l in range(CHUNK):
-                at = k * width + l * gases
-                spread_v[pl.ds((g * CHUNK + l) * rows, rows), at : at + gases] = part[g * rows : (g + 1) * rows]
-    coef_out[...] = spread_v[...].astype(jnp.bfloat16)
+    top_out[...] = jnp.broadcast_to(weight, (gpoints, columns))
+
+    def spread(parts, target):
+        for k, part in enumerate(parts):
+            for g in range(GROUPS):
+                for l in range(CHUNK):
+                    at = k * width + l * gases
+                    spread_v[pl.ds((g * CHUNK + l) * rows, rows), at : at + gases] = part[g * rows : (g + 1) * rows]
+        target[...] = spread_v[:, : target.shape[1]].astype(jnp.bfloat16)
+
+    absorbed = by_row[:, :gases]
+    parts = in_three(absorbed * (-LOG2E))
+    spread(parts, pass_out)
+    lane = lax.broadcasted_iota(jnp.int32, (gpoints, 16), 1)
+    logs = jnp.zeros((gpoints, 16), jnp.float32)
+    for k, part in enumerate(in_three(jnp.log(weight) * LOG2E)):
+        logs = jnp.where(lane == k, jnp.broadcast_to(part, logs.shape), logs)
+    for g in range(GROUPS):
+        for l in range(CHUNK):
+            spread_v[pl.ds((g * CHUNK + l) * rows, rows), 3 * width : 3 * width + 16] = logs[g * rows : (g + 1) * rows]
+    spread([absorbed] * 3, beam_out)
 
 
 def exchange(gas, layer_mass, column_state, absorption, single_scatter, solar_weight, subs):
@@ -95,25 +131,27 @@
             pltpu.VMEM((own, depth, columns), jnp.bfloat16),
             pltpu.VMEM((own, levels, columns), jnp.bfloat16),
             pltpu.VMEM((own, 2, columns), jnp.bfloat16),
+            pltpu.VMEM((3, own, depth, columns), jnp.bfloat16),
             pltpu.VMEM((CHUNK * gpoints, 3 * CHUNK * gases), jnp.bfloat16),
+            pltpu.VMEM((CHUNK * gpoints, 3 * CHUNK * gases + 16), jnp.bfloat16),
             pltpu.VMEM((gpoints, columns), jnp.float32),
             pltpu.VMEM((gpoints, columns), jnp.float32),
         ),
         in_specs=[anywhere] * 6,
-        out_specs=[vmem] * 6,
+        out_specs=[vmem] * 8,
         scratch_shapes=[
             pltpu.VMEM((gases, share), jnp.bfloat16),
             pltpu.VMEM((1, share), jnp.float32),
             pltpu.VMEM((1, share), jnp.float32),
             pltpu.VMEM((subs, 8, 128), jnp.float32),
             pltpu.VMEM((16, 128), jnp.float32),
-            pltpu.VMEM((CHUNK * gpoints, 3 * CHUNK * gases), jnp.float32),
+            pltpu.VMEM((CHUNK * gpoints, 3 * CHUNK * gases + 16), jnp.float32),
             pltpu.SemaphoreType.DMA((6,)),
             pltpu.SemaphoreType.DMA((subs,)),
             pltpu.SemaphoreType.DMA((subs,)),
         ],
         compiler_params=pltpu.CompilerParams(
-            collective_id=0, has_side_effects=True, vmem_limit_bytes=65100000
+            collective_id=0, has_side_effects=True, vmem_limit_bytes=61500000
         ),
         name="exchange_tables",
     )(gas, layer_mass, column_state, absorption.T, single_scatter.reshape(1, share), solar_weight.reshape(1, share))
@@ -121,9 +159,9 @@
 
 def kernel(
     own, levels, gases, columns, gpoints, subs,
-    gas_v, mass_v, state_v, coef_v, half_v, top_v, sunlit_hbm,
+    gas_v, mass_v, state_v, path_v, pass_coef, beam_coef, half_v, top_v, sunlit_hbm,
     heat_hbm, surf_hbm,
-    sunlit_s, depth_00, depth_01, depth_10, depth_11, pass_0, pass_1, upper_0, upper_1, lower_0, lower_1, net_0, net_v, flux_v, heat_v, surf_v,
+    sunlit_s, pass_00, pass_01, pass_10, pass_11, beam_00, beam_01, beam_10, beam_11, square_0, square_1, upper_0, upper_1, lower_0, lower_1, net_0, net_v, flux_v, heat_v, surf_v,
     in_sem, out_sem,
 ):
     band = lax.axis_index("band")
@@ -137,8 +175,9 @@
     lit_copy = pltpu.make_async_copy(sunlit_hbm, sunlit_s, in_sem.at[0])
     lit_copy.start()
 
-    depths = ((depth_00, depth_01), (depth_10, depth_11))
-    passes, uppers, lowers, nets = (pass_0, pass_1), (upper_0, upper_1), (lower_0, lower_1), (net_0, net_v)
+    passes = ((pass_00, pass_01), (pass_10, pass_11))
+    beams, squares = ((beam_00, beam_01), (beam_10, beam_11)), (square_0, square_1)
+    uppers, lowers, nets = (upper_0, upper_1), (lower_0, lower_1), (net_0, net_v)
 
     def state_row(j, k):
         row = state_v[j].astype(jnp.float32)[k : k + 1, :]
@@ -147,34 +186,34 @@
     def all_rows(row):
         return jnp.broadcast_to(row[None], (tiles, 8, columns)).reshape(rows, columns)
 
-    def optical(j, slot, g, i):
-        amounts = jnp.concatenate(
-            [gas_v[j, pl.ds(pl.multiple_of((i * dots + d) * width, width), width), :] for d in range(dots)], axis=1
-        )
+    def optical(j, g, at):
+        amounts = jnp.concatenate([gas_v[j, a, :] for a in at], axis=1)
         amounts = jnp.concatenate([amounts] * 3, axis=0)
-        return jnp.dot(coef_v[pl.ds(g * CHUNK * rows, CHUNK * rows), :], amounts, preferred_element_type=jnp.float32)
-
-    def keep(depth, slot, g, i):
+        return jnp.dot(pass_coef[pl.ds(g * CHUNK * rows, CHUNK * rows), :], amounts, preferred_element_type=jnp.float32)
+
+    def sunbeam(j, g, at):
+        path = [jnp.concatenate([path_v[k, j, a, :] for a in at], axis=1) for k in range(3)]
+        path = jnp.concatenate(path + [jnp.ones((16, dots * columns), jnp.bfloat16)], axis=0)
+        return jnp.dot(beam_coef[pl.ds(g * CHUNK * rows, CHUNK * rows), :], path, preferred_element_type=jnp.float32)
+
+    def prepare(make, targets, j, slot, g, i):
+        logs = make(j, g, [pl.ds(pl.multiple_of((i * dots + d) * width, width), width) for d in range(dots)])
         for d in range(dots):
             for m in range(CHUNK):
-                part = depth[m * rows : (m + 1) * rows, d * columns : (d + 1) * columns]
-                depths[slot][g][i * STEP + d * CHUNK + m] = part
-
-    def run(down, up, coming):
+                part = logs[m * rows : (m + 1) * rows, d * columns : (d + 1) * columns]
+                targets[slot][g][i * STEP + d * CHUNK + m] = part
+
+    def run(down, up, coming, late=None):
         start = ()
         if up is not None:
             ground = all_rows(state_row(up[0], 1))
             start += (ground, jnp.ones_like(ground))
         if down is not None:
-            mu = all_rows(state_row(down[0], 0))
-            slant = 1.0 / mu
-            top = top_v[pl.ds(down[2] * rows, rows), :] * mu
+            top = top_v[pl.ds(down[2] * rows, rows), :]
             start += (top, jnp.zeros_like(top))
 
         def body(i, carry):
             carry = list(carry)
-            if coming is not None:
-                ready = optical(*coming, i)
             if up is not None:
                 _, slot, g = up
                 upper, lower = carry[:2]
@@ -186,27 +225,29 @@
             for k in range(STEP):
                 if up is not None:
                     l = levels - 1 - (i * STEP + k)
-                    passing = jnp.exp2(depths[slot][g][l])
-                    passes[g][l] = passing
+                    passing = jnp.exp2(passes[slot][g][l])
+                    squares[g][l] = passing
                     square = passing * passing
                     reflected = half_up - half_up * square
-                    lower = lower - reflected * upper
-                    upper = reflected * lower + square * upper
+                    lower = 1.0 / (1.0 - reflected * upper)
+                    upper = reflected + (square * upper) * lower
                     uppers[g][l] = upper
                     lowers[g][l] = lower
                 if down is not None:
                     l = i * STEP + k
-                    below = lowers[g_d][l]
-                    inverse = 1.0 / below
-                    net = (below - uppers[g_d][l]) * (beam * inverse + scaled)
+                    inverse = lowers[g_d][l]
+                    net = (1.0 - uppers[g_d][l]) * (beam + scaled)
                     at = pl.ds(pl.multiple_of(l * 8, 8), 8)
                     net = jnp.sum(net.reshape(tiles, 8, columns), axis=0)
                     nets[g_d][at, :] = net if g_d == 0 else net + nets[0][at, :]
-                    beam_next = beam * jnp.exp2(depths[slot_d][g_d][l] * slant)
-                    scaled = passes[g_d][l] * scaled + (half_down * (beam - beam_next)) * inverse
+                    beam_next = jnp.exp2(beams[slot_d][g_d][l])
+                    scaled = (squares[g_d][l] * scaled + half_down * (beam - beam_next)) * inverse
                     beam = beam_next
             if coming is not None:
-                keep(ready, *coming[1:], i)
+                prepare(optical, passes, *coming, i)
+                prepare(sunbeam, beams, *coming, i)
+            if late is not None:
+                prepare(sunbeam, beams, *late, i)
             return (() if up is None else (upper, lower)) + (() if down is None else (beam, scaled))
 
         end = lax.fori_loop(0, steps, body, start)
@@ -230,18 +271,15 @@
         flux_v[pl.ds(levels, 1), :] = jnp.sum(net_v[at, :], axis=0, keepdims=True)
         below = flux_v[pl.ds(1, levels), :]
         lit = sunlit_s[(band * subs + sub) * own + j] == 1
-        heating = mass_v[j].astype(jnp.float32) * (here - below)
+        mu = state_row(j, 0)[:1]
+        heating = mass_v[j].astype(jnp.float32) * ((here - below) * mu)
         heat_v[j] = jnp.where(lit, heating, jnp.zeros_like(heating))
         heat_copy(j).start()
-        surface_down = jnp.sum(bottom, axis=0, keepdims=True)
+        surface_down = jnp.sum(bottom, axis=0, keepdims=True) * mu
         surf_v[pl.ds(j, 1), :] = jnp.where(lit, surface_down, jnp.zeros_like(surface_down))
 
-    def prepare(i, carry):
-        keep(optical(0, 0, 0, i), 0, 0, i)
-        return carry
-
-    lax.fori_loop(0, steps, prepare, 0)
-    run(None, (0, 0, 0), (0, 0, 1))
+    lax.fori_loop(0, steps, lambda i, c: (prepare(optical, passes, 0, 0, 0, i), c)[1], 0)
+    run(None, (0, 0, 0), (0, 0, 1), (0, 0, 0))
     lit_copy.wait()
 
     def pair(p, carry):
@@ -258,7 +296,7 @@
     run((j, 0, 0), (j, 0, 1), (j + 1, 1, 0))
     run((j, 0, 1), (j + 1, 1, 0), (j + 1, 1, 1))
     finish(j)
-    run((j + 1, 1, 0), (j + 1, 1, 1), None)
+    run((j + 1, 1, 0), (j + 1, 1, 1), (j + 1, 0, 0))
     run((j + 1, 1, 1), None, None)
     finish(j + 1)
     surf_copy = pltpu.make_async_copy(surf_v, surf_hbm, in_sem.at[1])
@@ -282,12 +320,12 @@
             jax.ShapeDtypeStruct((own, levels, columns), jnp.float32),
             jax.ShapeDtypeStruct((own, columns), jnp.float32),
         ),
-        in_specs=[pl.BlockSpec(memory_space=pltpu.VMEM)] * 6 + [anywhere],
+        in_specs=[pl.BlockSpec(memory_space=pltpu.VMEM)] * 8 + [anywhere],
         out_specs=[anywhere] * 2,
         scratch_shapes=[
             pltpu.SMEM((sunlit.shape[0],), jnp.int32),
         ]
-        + [per_level] * 10
+        + [per_level] * 14
         + [
             net, net,
             pltpu.VMEM((levels + 8, columns), jnp.float32),

time: 37.5 us -> 34.2 us (0.912)
  Pallas kernels: 36.7 us -> 33.4 us
    pallas_call x1, Pallas kernels: 27.5 us -> 23.8 us  [body(): pl.pallas_call(functools.partial(kernel, own, levels, gases, columns, gpo...]
where the time goes in v5:
time: 34.2 us; the launch traced here: 34 us
  Pallas kernels  33.4 us (98%)
  between operations  0.66 us (2%)
    pallas_call x1, Pallas kernels, body(): pl.pallas_call(functools.partial(kernel, own, levels, gases, columns, gpo...  23.8 us
    pallas_call x1, Pallas kernels, exchange(): pl.pallas_call(functools.partial(exchange_kernel, own, levels, gases, col...  9.57 us

profile of v5, /device:TPU:1, one launch (start us, length us, event | category | flops | bytes accessed | tf_op | source)
XLA Modules:
  0.0 34.0 jit_solution(4971937232294541166)
XLA Ops:
  0.6 0.0 copy-start
  0.6 9.6 %exchange_tables.1 = (bf16[8,512,128]{2,1,0:T(8,128)(2,1)S(1)}, bf16[8,64,128]{2,1,0:T(8,128)(2,1)S(1)}, bf16[8,2,128]{2,1,0:T(2,128)(2,1)S(1)}, bf16[3,8,512,12...) custom-call(bf16[64,512,128]{2,1,0:T(8,128)(2,1)} %bitcast.4, ...), custom_call_target="tpu_custom_call" | custom-call | tf_op jit(solution)/shard_map/exchange_tables/pallas_call | solution.py:128
  10.2 0.0 copy-done
  10.2 23.8 %solve_blocks.1 = (f32[8,64,128]{2,1,0:T(8,128)}, f32[8,128]{1,0:T(8,128)}) custom-call(bf16[8,512,128]{2,1,0:T(8,128)(2,1)S(1)} %get-tuple-element.10.gas_v, bf16[8,64,128]{2,1,0:T(8,128)(2,1)S(1)} %get-tuple-element.11.mass_v, bf16[8,2,128]{2,1,0:T(2,128)(2,1)S(1)} %get-tuple-element.12.state_v, bf16[3,8,512,128]{3,2,1,0:T(8,128)(2,1)S(1)} %get-tuple-element.13.path_v, ...), custom_call_target="tpu_custom_call" | custom-call | tf_op jit(solution)/shard_map/solve_blocks/pallas_call | solution.py:317
Async XLA Ops:
  0.6 9.6 %copy-start = (s32[1024]{0:T(1024)S(1)}, s32[1024]{0:T(1024)}, u32[]{:S(2)}) copy-start(s32[1024]{0:T(1024)} %sunlit_hbm.1) | copy-start | bytes 12292

commit v6 on v5

--- a/solution.py
+++ b/solution.py
@@ -25,7 +25,7 @@
     own, levels, gases, columns, share, subs,
     gas_hbm, mass_hbm, state_hbm, table_hbm, omega_hbm, weight_hbm,
     gas_out, mass_out, state_out, path_out, pass_out, beam_out, half_out, top_out,
-    table_v, omega_v, weight_v, pack_v, lay_v, spread_v, in_sem, send_sem, recv_sem,
+    table_v, omega_v, weight_v, lay_v, spread_v, in_sem, send_sem, recv_sem,
 ):
     band = lax.axis_index("band")
     sub = lax.axis_index("sub")
@@ -36,7 +36,7 @@
     for step in range(1, subs):
         pl.semaphore_signal(barrier, inc=1, device_id=(band, lax.rem(sub + step, subs)), device_id_type=MESH)
     tables = ((table_hbm, table_v), (omega_hbm, omega_v), (weight_hbm, weight_v))
-    copies = [pltpu.make_async_copy(source, target, in_sem.at[k]) for k, (source, target) in enumerate(tables)]
+    copies = [pltpu.make_async_copy(source, target.at[sub], in_sem.at[k]) for k, (source, target) in enumerate(tables)]
     blocks = ((gas_hbm, gas_out), (mass_hbm, mass_out), (state_hbm, state_out))
     others = [
         pltpu.make_async_copy(source.at[pl.ds(sub * own, own)], target, in_sem.at[3 + k])
@@ -48,22 +48,20 @@
     spread_v[...] = jnp.zeros_like(spread_v)
     for copy in copies:
         copy.wait()
-    pack_v[sub, 0:gases, 0:share] = table_v[...].astype(jnp.float32)
-    pack_v[sub, 0:1, 32 : 32 + share] = omega_v[...]
-    pack_v[sub, 0:1, 64 : 64 + share] = weight_v[...]
     pl.semaphore_wait(barrier, subs - 1)
     sent = []
     for step in range(1, subs):
-        copy = pltpu.make_async_remote_copy(
-            src_ref=pack_v.at[sub],
-            dst_ref=pack_v.at[sub],
-            send_sem=send_sem.at[step],
-            recv_sem=recv_sem.at[step],
-            device_id=(band, lax.rem(sub + step, subs)),
-            device_id_type=MESH,
-        )
-        copy.start()
-        sent.append(copy)
+        for k, (_, held) in enumerate(tables):
+            copy = pltpu.make_async_remote_copy(
+                src_ref=held.at[sub],
+                dst_ref=held.at[sub],
+                send_sem=send_sem.at[step, k],
+                recv_sem=recv_sem.at[step, k],
+                device_id=(band, lax.rem(sub + step, subs)),
+                device_id_type=MESH,
+            )
+            copy.start()
+            sent.append(copy)
     for copy in others:
         copy.wait()
 
@@ -90,9 +88,9 @@
 
     for s in range(subs):
         at = slice(s * share, (s + 1) * share)
-        lay_v[0:gases, at] = pack_v[s, 0:gases, 0:share]
-        lay_v[gases : gases + 1, at] = pack_v[s, 0:1, 32 : 32 + share]
-        lay_v[gases + 1 : gases + 2, at] = pack_v[s, 0:1, 64 : 64 + share]
+        lay_v[0:gases, at] = table_v[s].astype(jnp.float32)
+        lay_v[gases : gases + 1, at] = omega_v[s]
+        lay_v[gases + 1 : gases + 2, at] = weight_v[s]
     by_row = jnp.transpose(lay_v[...])[:gpoints]
     weight = by_row[:, gases + 1 : gases + 2]
     half_out[...] = jnp.broadcast_to(0.5 * by_row[:, gases : gases + 1], (gpoints, columns))
@@ -140,15 +138,14 @@
         in_specs=[anywhere] * 6,
         out_specs=[vmem] * 8,
         scratch_shapes=[
-            pltpu.VMEM((gases, share), jnp.bfloat16),
-            pltpu.VMEM((1, share), jnp.float32),
-            pltpu.VMEM((1, share), jnp.float32),
-            pltpu.VMEM((subs, 8, 128), jnp.float32),
+            pltpu.VMEM((subs, gases, share), jnp.bfloat16),
+            pltpu.VMEM((subs, 1, share), jnp.float32),
+            pltpu.VMEM((subs, 1, share), jnp.float32),
             pltpu.VMEM((16, 128), jnp.float32),
             pltpu.VMEM((CHUNK * gpoints, 3 * CHUNK * gases + 16), jnp.float32),
             pltpu.SemaphoreType.DMA((6,)),
-            pltpu.SemaphoreType.DMA((subs,)),
-            pltpu.SemaphoreType.DMA((subs,)),
+            pltpu.SemaphoreType.DMA((subs, 3)),
+            pltpu.SemaphoreType.DMA((subs, 3)),
         ],
         compiler_params=pltpu.CompilerParams(
             collective_id=0, has_side_effects=True, vmem_limit_bytes=61500000

time: 34.2 us -> 34.4 us (level)
  no operation moved by 1% of the time
where the time goes in v6:
time: 34.4 us; the launch traced here: 34.3 us
  Pallas kernels  33.6 us (98%)
  between operations  0.66 us (2%)
    pallas_call x1, Pallas kernels, body(): pl.pallas_call(functools.partial(kernel, own, levels, gases, columns, gpo...  23.8 us
    pallas_call x1, Pallas kernels, exchange(): pl.pallas_call(functools.partial(exchange_kernel, own, levels, gases, col...  9.84 us

profile of v6, /device:TPU:1, one launch (start us, length us, event | category | flops | bytes accessed | tf_op | source)
XLA Modules:
  0.0 34.3 jit_solution(2716655332661909927)
XLA Ops:
  0.6 0.0 copy-start
  0.6 9.8 %exchange_tables.1 = (bf16[8,512,128]{2,1,0:T(8,128)(2,1)S(1)}, bf16[8,64,128]{2,1,0:T(8,128)(2,1)S(1)}, bf16[8,2,128]{2,1,0:T(2,128)(2,1)S(1)}, bf16[3,8,512,12...) custom-call(bf16[64,512,128]{2,1,0:T(8,128)(2,1)} %bitcast.4, ...), custom_call_target="tpu_custom_call" | custom-call | tf_op jit(solution)/shard_map/exchange_tables/pallas_call | solution.py:126
  10.5 0.0 copy-done
  10.5 23.8 %solve_blocks.1 = (f32[8,64,128]{2,1,0:T(8,128)}, f32[8,128]{1,0:T(8,128)}) custom-call(bf16[8,512,128]{2,1,0:T(8,128)(2,1)S(1)} %get-tuple-element.10.gas_v, bf16[8,64,128]{2,1,0:T(8,128)(2,1)S(1)} %get-tuple-element.11.mass_v, bf16[8,2,128]{2,1,0:T(2,128)(2,1)S(1)} %get-tuple-element.12.state_v, bf16[3,8,512,128]{3,2,1,0:T(8,128)(2,1)S(1)} %get-tuple-element.13.path_v, ...), custom_call_target="tpu_custom_call" | custom-call | tf_op jit(solution)/shard_map/solve_blocks/pallas_call | solution.py:314
Async XLA Ops:
  0.6 9.9 %copy-start = (s32[1024]{0:T(1024)S(1)}, s32[1024]{0:T(1024)}, u32[]{:S(2)}) copy-start(s32[1024]{0:T(1024)} %sunlit_hbm.1) | copy-start | bytes 12292
